TPU v7x, 32 devices: a whole 2x2x4 slice. The times are simulated.
32 devices in a mesh: gx: 4 (over y, x), gy: 2 (over core), gz: 4 (over z).
Axes of the slice: x: 2, y: 2, z: 4, core: 2. Of those that a mesh axis runs over, the one named last changes fastest.
Arguments:
- energy: float32 [128, 256, 256], P(('gz', 'gy', 'gx')), may hold values from -5 to 5
- flow: float32 [4, 128, 256, 256], P(None, ('gz', 'gy', 'gx')), may hold values from -0.1 to 0.12, as said below
Outputs:
- energy_next: float32 [128, 256, 256], P('gz', 'gx', 'gy')
- plane_mean: float32 [128], P('gz')
- running_mean: float32 [128], P('gz')
Inputs may be any that keep to these rules, and one draw needn't show every extreme that they name: flow[0], flow[1] and flow[2] lie within -0.1 to 0.1; flow[3] lies within 0.02 to 0.12.
All inputs are finite; a program needn't handle non-finite values.
Results may differ from a plain program's by a relative error of at most 0.00002.
Values sent between devices are 32-bit elements; how exact they have to be, the bound alone decides.
A program may use at most 128 MiB of HBM per device.

v0:
```python
import functools

import jax
import jax.numpy as jnp
from jax import lax
from jax.experimental import pallas as pl
from jax.experimental.pallas import tpu as pltpu
from jax.sharding import PartitionSpec as P

MESH = pl.DeviceIdType.MESH
PAD = 8
ROWS = 16
STRIP = 32


def shifted(block, rows):
    size = block.shape[0]
    return (
        block[PAD : PAD + rows],
        pltpu.roll(block, size - 1, 0)[PAD : PAD + rows],
        pltpu.roll(block, 1, 0)[PAD : PAD + rows],
    )


def sideways(block, lane):
    width = block.shape[1]
    right = jnp.where(lane == width - 1, 0.0, pltpu.roll(block, width - 1, 1))
    left = jnp.where(lane == 0, 0.0, pltpu.roll(block, 1, 1))
    return right, left


def above(k, k_up, speed, e, e_up):
    return (0.5 * (k + k_up) - jnp.minimum(speed, 0.0)) * (e_up - e)


def below(k, k_down, speed, e, e_down):
    return (0.5 * (k + k_down) + jnp.maximum(speed, 0.0)) * (e_down - e)


def kernel(
    sizes, e_hbm, f_hbm, out, mean_ref, run_ref,
    e_v, k_v, u_v, h_v, n_v, group_v, block_v,
    load_sem, s1, r1, s2, r2, s3, r3, own_sem, s4, r4, s5, r5,
):
    gx_n, gy_n, gz_n, planes, nx, ny = sizes
    height, width = nx // gx_n, ny // gy_n
    gx, gy, gz = lax.axis_index("gx"), lax.axis_index("gy"), lax.axis_index("gz")
    peers = gx_n * gy_n
    place = gy * gx_n + gx
    slab = gz * peers + place

    def device(number):
        return {
            "gx": lax.rem(number, gx_n),
            "gy": lax.rem(lax.div(number, gx_n), gy_n),
            "gz": lax.div(number, peers),
        }

    total = peers * gz_n
    up = device(lax.rem(slab + 1, total))
    down = device(lax.rem(slab + total - 1, total))

    def peer(step):
        return {
            "gx": lax.rem(place + step, gx_n) if gy_n == 1 else lax.rem(lax.rem(place + step, peers), gx_n),
            "gy": lax.div(lax.rem(place + step, peers), gx_n),
            "gz": gz,
        }

    def layer(step):
        return {"gx": gx, "gy": gy, "gz": lax.rem(gz + step, gz_n)}

    loads = [
        pltpu.make_async_copy(e_hbm, e_v.at[pl.ds(1, planes), pl.ds(PAD, nx)], load_sem.at[0]),
        pltpu.make_async_copy(f_hbm.at[3], k_v.at[pl.ds(1, planes), pl.ds(PAD, nx)], load_sem.at[1]),
        pltpu.make_async_copy(f_hbm.at[pl.ds(0, 3)], u_v, load_sem.at[2]),
    ]

    barrier = pltpu.get_barrier_semaphore()
    greet = [up, down] + [peer(i) for i in range(1, peers)] + [layer(i) for i in range(1, gz_n)]
    for target in greet:
        pl.semaphore_signal(barrier, inc=1, device_id=target, device_id_type=MESH)
    for load in loads:
        load.start()
    edge = jnp.zeros((planes, PAD, ny), jnp.float32)
    for ref in (e_v, k_v, h_v):
        ref[1 : planes + 1, 0:PAD, :] = edge
        ref[1 : planes + 1, PAD + nx : PAD + nx + PAD, :] = edge
    pl.semaphore_wait(barrier, len(greet))

    def lanes(c):
        return pl.ds(c * width, width)

    def send(src, dst, send_sem, recv_sem, target):
        return pltpu.make_async_remote_copy(
            src_ref=src, dst_ref=dst, send_sem=send_sem, recv_sem=recv_sem,
            device_id=target, device_id_type=MESH,
        )

    first = []
    rows_all = pl.ds(PAD, nx)
    for c in range(gy_n):
        copies = [
            send(e_hbm.at[planes - 1, :, lanes(c)], e_v.at[0, rows_all, lanes(c)], s1.at[c, 0], r1.at[c, 0], up),
            send(e_hbm.at[0, :, lanes(c)], e_v.at[planes + 1, rows_all, lanes(c)], s1.at[c, 1], r1.at[c, 1], down),
            send(f_hbm.at[3, planes - 1, :, lanes(c)], k_v.at[0, rows_all, lanes(c)], s1.at[c, 2], r1.at[c, 2], up),
            send(f_hbm.at[3, 0, :, lanes(c)], k_v.at[planes + 1, rows_all, lanes(c)], s1.at[c, 3], r1.at[c, 3], down),
        ]
        for copy in copies:
            copy.start()
        first.append(copies)

    for load in loads:
        load.wait()

    lane = lax.broadcasted_iota(jnp.int32, (ROWS, ny), 1)

    def local(src, p, r):
        start = pl.multiple_of(r * ROWS, ROWS)
        here = pl.ds(start, ROWS)
        inner = pl.ds(pl.multiple_of(start + PAD, PAD), ROWS)
        tall = pl.ds(start, ROWS + 2 * PAD)
        e, e_next, e_prev = shifted(src[p + 1, tall, :], ROWS)
        k, k_next, k_prev = shifted(k_v[p + 1, tall, :], ROWS)
        speed = u_v[1, p, here, :]
        value = e + above(k, k_next, speed, e, e_next) + below(k, k_prev, speed, e, e_prev)
        e_next, e_prev = sideways(e, lane)
        k_next, k_prev = sideways(k, lane)
        speed = u_v[2, p, here, :]
        value = value + above(k, k_next, speed, e, e_next) + below(k, k_prev, speed, e, e_prev)
        speed = u_v[0, p, here, :]
        if p < planes - 1:
            value = value + above(k, k_v[p + 2, inner, :], speed, e, src[p + 2, inner, :])
        if p > 0:
            value = value + below(k, k_v[p, inner, :], speed, e, src[p, inner, :])
        return here, inner, value

    def edge_terms(src, c, r):
        start = pl.multiple_of(r * STRIP, STRIP)
        here = pl.ds(start, STRIP)
        inner = pl.ds(pl.multiple_of(start + PAD, PAD), STRIP)
        at = lanes(c)
        top = above(
            k_v[planes, inner, at], k_v[planes + 1, inner, at], u_v[0, planes - 1, here, at],
            src[planes, inner, at], src[planes + 1, inner, at],
        )
        bottom = below(
            k_v[1, inner, at], k_v[0, inner, at], u_v[0, 0, here, at], src[1, inner, at], src[0, inner, at]
        )
        return here, inner, top, bottom

    def folded(value):
        rows = value.shape[0]
        part = value[0:8]
        for i in range(8, rows, 8):
            part = part + value[i : i + 8]
        return part

    for p in range(planes):

        @pl.loop(0, nx // ROWS)
        def _(r, p=p):
            here, inner, value = local(e_v, p, r)
            h_v[p + 1, inner, :] = value

    second = []
    for c in range(gy_n):
        for copy in first[c]:
            copy.wait_recv()

        @pl.loop(0, nx // STRIP)
        def _(r, c=c):
            here, inner, top, bottom = edge_terms(e_v, c, r)
            h_v[planes, inner, lanes(c)] = h_v[planes, inner, lanes(c)] + top
            h_v[1, inner, lanes(c)] = h_v[1, inner, lanes(c)] + bottom

        copies = [
            send(h_v.at[planes, rows_all, lanes(c)], h_v.at[0, rows_all, lanes(c)], s2.at[c, 0], r2.at[c, 0], up),
            send(h_v.at[1, rows_all, lanes(c)], h_v.at[planes + 1, rows_all, lanes(c)], s2.at[c, 1], r2.at[c, 1], down),
        ]
        for copy in copies:
            copy.start()
        second.append(copies)

    sums = []
    for p in range(planes):

        def body(r, carry, p=p):
            here, inner, value = local(h_v, p, r)
            n_v[p, here, :] = value
            return carry + folded(value)

        sums.append(lax.fori_loop(0, nx // ROWS, body, jnp.zeros((8, ny), jnp.float32)))

    def hand_out(c, p0, count, part):
        for d in range(gx_n):
            to = lax.rem(gx + d, gx_n)
            src = n_v.at[pl.ds(p0, count), pl.ds(pl.multiple_of(to * height, 8), height), lanes(c)]
            dst = out.at[pl.ds(place * planes + p0, count)]
            if d == 0:

                @pl.when(gy == c)
                def _():
                    pltpu.make_async_copy(src, dst, own_sem.at[part]).start()

                @pl.when(gy != c)
                def _():
                    send(src, dst, s3.at[c * gx_n + d, part], r3.at[place, part],
                         {"gx": gx, "gy": jnp.int32(c), "gz": gz}).start()
            else:
                send(src, dst, s3.at[c * gx_n + d, part], r3.at[place, part],
                     {"gx": to, "gy": jnp.int32(c), "gz": gz}).start()

    parts = []
    if planes > 2:
        parts.append((1, planes - 2))
        for c in range(gy_n):
            hand_out(c, 1, planes - 2, 0)
    outer = sorted({0, planes - 1})
    first_outer = len(parts)
    parts += [(p, 1) for p in outer]

    extra = [jnp.zeros((8, width), jnp.float32), jnp.zeros((8, width), jnp.float32)]
    for c in range(gy_n):
        for copy in second[c]:
            copy.wait_recv()

        def body(r, carry, c=c):
            here, inner, top, bottom = edge_terms(h_v, c, r)
            n_v[planes - 1, here, lanes(c)] = n_v[planes - 1, here, lanes(c)] + top
            n_v[0, here, lanes(c)] = n_v[0, here, lanes(c)] + bottom
            return carry[0] + folded(top), carry[1] + folded(bottom)

        extra = lax.fori_loop(0, nx // STRIP, body, tuple(extra))
        for part, p in enumerate(outer):
            hand_out(c, p, 1, first_outer + part)

    spot = lax.broadcasted_iota(jnp.int32, (8, 128), 1)
    mine = jnp.zeros((8, 128), jnp.float32)
    for p in range(planes):
        amount = jnp.sum(sums[p], keepdims=True)
        if p == planes - 1:
            amount = amount + jnp.sum(extra[0], keepdims=True)
        if p == 0:
            amount = amount + jnp.sum(extra[1], keepdims=True)
        mine = jnp.where(spot == place * planes + p, amount * (1.0 / (nx * ny)), mine)
    group_v[0] = mine
    share = []
    for i in range(1, peers):
        copy = send(group_v.at[0], group_v.at[i], s4.at[i], r4.at[i], peer(i))
        copy.start()
        share.append(copy)
    for copy in share:
        copy.wait_recv()
    means = mine
    for i in range(1, peers):
        means = means + group_v[i]
    block_v[0] = means
    climb = []
    for i in range(1, gz_n):
        copy = send(block_v.at[0], block_v.at[i], s5.at[i], r5.at[i], layer(i))
        copy.start()
        climb.append(copy)
    running = means
    step = 1
    while step < peers * planes:
        running = running + jnp.where(spot >= step, pltpu.roll(running, step, 1), 0.0)
        step *= 2
    mean_ref[...] = means
    for copy in climb:
        copy.wait_recv()
    lower = jnp.zeros((8, 128), jnp.float32)
    for i in range(1, gz_n):
        lower = lower + jnp.where(gz >= i, block_v[i], 0.0)
    offset = jnp.sum(lower[0:1], axis=1, keepdims=True)
    rank = (gz * peers * planes + spot + 1).astype(jnp.float32)
    run_ref[...] = (running + offset) / rank

    for part, (p0, count) in enumerate(parts):
        for d in range(peers):
            source = lax.rem(place + d, peers)
            dst = out.at[pl.ds(source * planes + p0, count)]
            src = n_v.at[pl.ds(p0, count), pl.ds(0, height), pl.ds(0, width)]
            if d == 0:
                pltpu.make_async_copy(src, dst, own_sem.at[part]).wait()
            else:
                send(src, dst, s3.at[0, part], r3.at[source, part], peer(d)).wait_recv()
        for c in range(gy_n):
            for d in range(gx_n):
                copy = send(
                    n_v.at[pl.ds(p0, count), pl.ds(0, height), pl.ds(0, width)],
                    out.at[pl.ds(p0, count)], s3.at[c * gx_n + d, part], r3.at[0, part], up,
                )
                if d == 0:

                    @pl.when(gy != c)
                    def _():
                        copy.wait_send()
                else:
                    copy.wait_send()
    for copies in first + second + [share, climb]:
        for copy in copies:
            copy.wait_send()


def split_kernel(
    sizes, e_hbm, f_hbm, out, corr, mean_ref, run_ref,
    e_v, k_v, u_v, h_v, n_v, g_v, rx_v, d_v, c_v, near_v, far_v, group_v, block_v,
    load_sem, s1, r1, s2, r2, s3, r3, sc, rc, s4, r4, s5, r5,
):
    gx_n, gy_n, gz_n, planes, nx, ny = sizes
    height, width = nx // gx_n, ny // gy_n
    halves = gx_n // 2
    gx, gy, gz = lax.axis_index("gx"), lax.axis_index("gy"), lax.axis_index("gz")
    peers = gx_n * gy_n
    count = peers * planes
    place = gy * gx_n + gx
    slab = gz * peers + place
    parity = lax.rem(gx, 2)
    total = peers * gz_n
    above_slab, below_slab = lax.rem(slab + 1, total), lax.rem(slab + total - 1, total)
    last = planes - 1
    own_plane = (0, last)

    def device(number):
        return {
            "gx": lax.rem(number, gx_n),
            "gy": lax.rem(lax.div(number, gx_n), gy_n),
            "gz": lax.div(number, peers),
        }

    neighbour = (device(below_slab), device(above_slab))

    def peer(step):
        return device(gz * peers + lax.rem(place + step, peers))

    def layer(step):
        return {"gx": gx, "gy": gy, "gz": lax.rem(gz + step, gz_n)}

    loads = [
        pltpu.make_async_copy(e_hbm, e_v.at[:, pl.ds(PAD, nx)], load_sem.at[0]),
        pltpu.make_async_copy(f_hbm.at[3], k_v.at[:, pl.ds(PAD, nx)], load_sem.at[1]),
        pltpu.make_async_copy(f_hbm.at[pl.ds(0, 3)], u_v, load_sem.at[2]),
    ]
    for load in loads:
        load.start()

    barrier = pltpu.get_barrier_semaphore()
    greet = list(neighbour) + [peer(i) for i in range(1, peers)] + [layer(i) for i in range(1, gz_n)]
    greet.append(device(lax.rem(gz + gz_n - 1, gz_n) * peers + peers - 1))
    greet.append(device(lax.rem(gz + 1, gz_n) * peers))
    for target in greet:
        pl.semaphore_signal(barrier, inc=1, device_id=target, device_id_type=MESH)
    edge = jnp.zeros((planes, PAD, ny), jnp.float32)
    for ref in (e_v, k_v, h_v):
        ref[:, 0:PAD, :] = edge
        ref[:, PAD + nx : PAD + nx + PAD, :] = edge
    outermost = (place == 0).astype(jnp.int32) + (place == peers - 1).astype(jnp.int32)
    pl.semaphore_wait(barrier, len(greet) - 2 + outermost * peers)

    def lanes(c):
        return pl.ds(c * width, width)

    def send(src, dst, send_sem, recv_sem, target):
        return pltpu.make_async_remote_copy(
            src_ref=src, dst_ref=dst, send_sem=send_sem, recv_sem=recv_sem,
            device_id=target, device_id_type=MESH,
        )

    def row(block, extra=0):
        return pl.multiple_of(block * height + extra, 8)

    mine = [2 * j + parity for j in range(halves)]
    theirs = [2 * j + 1 - parity for j in range(halves)]

    first = {}

    def start_first(j, fields):
        for f in (1, 0):
            p, rows = own_plane[f], pl.ds(row(theirs[j]), height)
            inner = pl.ds(row(theirs[j], PAD), height)
            sources = (e_hbm.at[p, rows], f_hbm.at[3, p, rows], g_v.at[f, rows], h_v.at[p, inner])
            for i in fields:
                copy = send(sources[i], rx_v.at[1 - f, i, j], s1.at[f, i, j], r1.at[1 - f, i, j], neighbour[f])
                copy.start()
                first[f, i, j] = copy

    start_first(0, (0, 1))
    for load in loads:
        load.wait()

    lane = lax.broadcasted_iota(jnp.int32, (ROWS, ny), 1)
    tiles = height // ROWS

    def local(src, p, start):
        here = pl.ds(start, ROWS)
        inner = pl.ds(pl.multiple_of(start + PAD, 8), ROWS)
        tall = pl.ds(start, ROWS + 2 * PAD)
        e, e_next, e_prev = shifted(src[p, tall, :], ROWS)
        k, k_next, k_prev = shifted(k_v[p, tall, :], ROWS)
        speed = u_v[1, p, here, :]
        value = e + above(k, k_next, speed, e, e_next) + below(k, k_prev, speed, e, e_prev)
        e_next, e_prev = sideways(e, lane)
        k_next, k_prev = sideways(k, lane)
        speed = u_v[2, p, here, :]
        value = value + above(k, k_next, speed, e, e_next) + below(k, k_prev, speed, e, e_prev)
        speed = u_v[0, p, here, :]
        if p < last:
            value = value + above(k, k_v[p + 1, inner, :], speed, e, src[p + 1, inner, :])
        if p > 0:
            value = value + below(k, k_v[p - 1, inner, :], speed, e, src[p - 1, inner, :])
        return here, inner, value, 0.5 * k, speed

    def folded(value):
        part = value[0:8]
        for i in range(8, value.shape[0], 8):
            part = part + value[i : i + 8]
        return part

    def first_step(block, which):
        @pl.loop(0, tiles)
        def _(t):
            start = pl.multiple_of(block * height + t * ROWS, 8)
            for p in which:
                here, inner, value, half, speed = local(e_v, p, start)
                h_v[p, inner, :] = value
                if p == 0:
                    g_v[0, here, :] = half + jnp.maximum(speed, 0.0)
                if p == last:
                    g_v[1, here, :] = half - jnp.minimum(speed, 0.0)

    for j in range(halves):
        if j > 0:
            start_first(j, (0, 1))
        first_step(theirs[j], own_plane)
        start_first(j, (2, 3))
    for j in range(halves):
        first_step(mine[j], own_plane)
    inside = tuple(range(1, last))
    if inside:
        for block in range(gx_n):
            first_step(block, inside)

    second, fixes = [], []
    side_slab = (below_slab, above_slab)
    zero = jnp.zeros((8, ny), jnp.float32)
    spill = (zero, zero)
    sums = [zero] * planes

    def second_step(block, j, own, p, low, high):
        def body(t, carry):
            start = pl.multiple_of(block * height + t * ROWS, 8)
            at = pl.ds(pl.multiple_of(t * ROWS, 8), ROWS)
            here, inner, value, half, speed = local(h_v, p, start)
            for f in (0, 1):
                if own and p == own_plane[f]:
                    value = value + near_v[f, j, at, :]
            n_v[p, here, :] = value
            return carry + folded(value)

        sums[p] = lax.fori_loop(low, high, body, sums[p])

    def ahead(j):
        for p in range(planes):
            inside = 0 < p < last
            second_step(mine[j], j, 1, p, 0 if inside else 1, tiles if inside else tiles - 1)

    def behind(j):
        for p in own_plane:
            for t in sorted({0, tiles - 1}):
                second_step(mine[j], j, 1, p, t, t + 1)

    for j in range(halves):
        for f in (0, 1):
            for i in range(4):
                send(rx_v.at[f, i, j], rx_v.at[f, i, j], s1.at[f, i, j], r1.at[f, i, j], neighbour[f]).wait_recv()

        def body(t, carry, j=j):
            sums = []
            at = pl.ds(pl.multiple_of(t * ROWS, 8), ROWS)
            start = pl.multiple_of(mine[j] * height + t * ROWS, 8)
            here, inner = pl.ds(start, ROWS), pl.ds(pl.multiple_of(start + PAD, 8), ROWS)
            for f in (0, 1):
                p = own_plane[f]
                to_near = g_v[f, here, :] + 0.5 * rx_v[f, 1, j, at, :]
                to_far = rx_v[f, 2, j, at, :] + 0.5 * k_v[p, inner, :]
                step = rx_v[f, 0, j, at, :] - e_v[p, inner, :]
                push = to_far * step
                d_v[f, j, at, :] = -push
                here_half = h_v[p, inner, :] + to_near * step
                far_half = rx_v[f, 3, j, at, :] - push
                h_v[p, inner, :] = here_half
                step = far_half - here_half
                near_v[f, j, at, :] = to_near * step
                fix = -(to_far * step)
                far_v[f, j, at, :] = fix
                sums.append(carry[f] + folded(fix))
            return tuple(sums)

        spill = lax.fori_loop(0, tiles, body, spill)
        for f in (1, 0):
            copy = send(d_v.at[f, j], c_v.at[1 - f, j], s2.at[f, j], r2.at[1 - f, j], neighbour[f])
            copy.start()
            second.append(copy)
        if j < halves - 1:
            ahead(j)

    def fix_copies(act):
        for j in range(halves):
            for f in (0, 1):
                far_place, far_block = lax.rem(side_slab[f], peers), lax.div(side_slab[f], peers)
                slot = lax.div(far_place, 2)
                for c in range(gy_n):
                    at_home = (mine[j] == gx) & (gy == c) & (far_block == gz)
                    act(
                        at_home, far_v.at[f, j, :, lanes(c)], corr.at[slot, 1 - f], sc.at[f, j, c],
                        rc.at[slot, 1 - f], {"gx": mine[j], "gy": jnp.int32(c), "gz": far_block},
                    )

    def begin(at_home, src, dst, send_sem, recv_sem, target):
        @pl.when(at_home)
        def _():
            pltpu.make_async_copy(src, dst, recv_sem).start()

        @pl.when(jnp.logical_not(at_home))
        def _():
            send(src, dst, send_sem, recv_sem, target).start()

    def finish(at_home, src, dst, send_sem, recv_sem, target):
        @pl.when(jnp.logical_not(at_home))
        def _():
            send(src, dst, send_sem, recv_sem, target).wait_send()

    fix_copies(begin)
    ahead(halves - 1)

    def hand_out(block, j, own, act):
        for c in range(gy_n):
            at_home = (block == gx) & (gy == c)
            act(
                at_home, n_v.at[:, pl.ds(row(block), height), lanes(c)], out.at[pl.ds(place * planes, planes)],
                s3.at[2 * j + own, c], r3.at[place], {"gx": block, "gy": jnp.int32(c), "gz": gz},
            )

    for j in range(halves):
        for f in (0, 1):
            first[f, 3, j].wait_send()
            send(d_v.at[f, j], c_v.at[f, j], s2.at[f, j], r2.at[f, j], neighbour[f]).wait_recv()

        @pl.loop(0, tiles)
        def _(t, j=j):
            at = pl.ds(pl.multiple_of(t * ROWS, 8), ROWS)
            inner = pl.ds(pl.multiple_of(theirs[j] * height + t * ROWS + PAD, 8), ROWS)
            for f in (0, 1):
                h_v[own_plane[f], inner, :] = h_v[own_plane[f], inner, :] + c_v[f, j, at, :]

        for p in range(planes):
            second_step(theirs[j], j, 0, p, 0, tiles)
        if j < halves - 1:
            hand_out(theirs[j], j, 0, begin)
    for j in range(halves):
        behind(j)

    spot = lax.broadcasted_iota(jnp.int32, (8, 128), 1)
    scale = 1.0 / (nx * ny)
    part = jnp.zeros((8, 128), jnp.float32)
    base = place * planes
    amounts = [jnp.sum(spill[0], keepdims=True)] + [jnp.sum(s, keepdims=True) for s in sums]
    amounts.append(jnp.sum(spill[1], keepdims=True))
    for i, amount in enumerate(amounts):
        part = jnp.where(spot == base + i, amount * scale, part)
    group_v[0] = part
    share = []
    for i in range(1, peers):
        copy = send(group_v.at[0], group_v.at[i], s4.at[i], r4.at[i], peer(i))
        copy.start()
        share.append(copy)
    hand_out(theirs[-1], halves - 1, 0, begin)
    for j in range(halves):
        hand_out(mine[j], j, 1, begin)
    for copy in share:
        copy.wait_recv()
    for i in range(1, peers):
        part = part + group_v[i]
    block_v[0] = part
    climb = []
    for i in range(1, gz_n):
        copy = send(block_v.at[0], block_v.at[i], s5.at[i], r5.at[i], layer(i))
        copy.start()
        climb.append(copy)
    for copy in climb:
        copy.wait_recv()
    lower = jnp.zeros((8, 128), jnp.float32)
    own_lane = (spot >= 1) & (spot <= count)
    means = jnp.where(own_lane, part, 0.0)
    for i in range(gz_n):
        vector = block_v[i]
        block = lax.rem(gz + gz_n - i, gz_n)
        owner = jnp.where(own_lane, block, jnp.where(
            spot == 0, lax.rem(block + gz_n - 1, gz_n), lax.rem(block + 1, gz_n)))
        vector = jnp.where(spot <= count + 1, vector, 0.0)
        lower = lower + jnp.where(owner < gz, vector, 0.0)
        low = jnp.sum(jnp.where((spot == 0) & (owner == gz), vector, 0.0)[0:1], axis=1, keepdims=True)
        high = jnp.sum(jnp.where((spot == count + 1) & (owner == gz), vector, 0.0)[0:1], axis=1, keepdims=True)
        means = means + jnp.where(spot == count, low, 0.0) + jnp.where(spot == 1, high, 0.0)
    means = pltpu.roll(means, 127, 1)
    running = means
    step = 1
    while step < count:
        running = running + jnp.where(spot >= step, pltpu.roll(running, step, 1), 0.0)
        step *= 2
    mean_ref[...] = means
    offset = jnp.sum(lower[0:1], axis=1, keepdims=True)
    rank = (gz * count + spot + 1).astype(jnp.float32)
    run_ref[...] = (running + offset) / rank

    for s in range(peers):
        dst = out.at[pl.ds(s * planes, planes)]
        send(dst, dst, s3.at[0, 0], r3.at[s], neighbour[0]).wait_recv()
    for slot in range(peers // 2):
        for f in (0, 1):
            send(corr.at[slot, f], corr.at[slot, f], sc.at[0, 0, 0], rc.at[slot, f], neighbour[0]).wait_recv()
    for j in range(halves):
        hand_out(theirs[j], j, 0, finish)
        hand_out(mine[j], j, 1, finish)
    fix_copies(finish)
    for key, copy in first.items():
        if key[1] != 3:
            copy.wait_send()
    for copy in second + share + climb:
        copy.wait_send()


def finish_kernel(planes, base_ref, corr_ref, mean_in, run_in, out_ref, mean_ref, run_ref, fix_v, done):
    other = 1 - lax.rem(lax.axis_index("gx"), 2)
    copies = []
    for slot in range(corr_ref.shape[0]):
        whole = pl.ds((2 * slot + 1 - other) * planes, planes)
        copies.append(pltpu.make_async_copy(base_ref.at[whole], out_ref.at[whole], done.at[slot, 0]))
        copies[-1].start()
    for slot in range(corr_ref.shape[0]):
        start = (2 * slot + other) * planes
        fix_v[slot] = base_ref[pl.ds(start, planes)]
        for f, p in ((0, 0), (1, planes - 1)):
            fix_v[slot, p] = fix_v[slot, p] + corr_ref[slot, f]
        copies.append(pltpu.make_async_copy(fix_v.at[slot], out_ref.at[pl.ds(start, planes)], done.at[slot, 1]))
        copies[-1].start()
    count = mean_ref.shape[0]
    mean_ref[...] = mean_in[0, 0:count]
    run_ref[...] = run_in[0, 0:count]
    for copy in copies:
        copy.wait()


def by_parity(energy, flow):
    gx_n, gy_n, gz_n = (lax.axis_size(a) for a in ("gx", "gy", "gz"))
    planes, nx, ny = energy.shape
    peers, halves = gx_n * gy_n, gx_n // 2
    height, width = nx // gx_n, ny // gy_n
    dma = pltpu.SemaphoreType.DMA
    f32 = jnp.float32
    anywhere = pl.BlockSpec(memory_space=pl.ANY)
    vmem = pl.BlockSpec(memory_space=pltpu.VMEM)
    tall = pltpu.VMEM((planes, nx + 2 * PAD, ny), f32)
    hbm = pl.BlockSpec(memory_space=pltpu.HBM)
    faces = pltpu.VMEM((2, halves, height, ny), f32)
    energy, flow = (pltpu.with_memory_space_constraint(x, pltpu.HBM) for x in (energy, flow))
    base, corr, means, running = pl.pallas_call(
        functools.partial(split_kernel, (gx_n, gy_n, gz_n, planes, nx, ny)),
        out_shape=(
            jax.ShapeDtypeStruct((planes * peers, height, width), f32),
            jax.ShapeDtypeStruct((peers // 2, 2, height, width), f32),
            jax.ShapeDtypeStruct((8, 128), f32),
            jax.ShapeDtypeStruct((8, 128), f32),
        ),
        in_specs=[hbm, hbm],
        out_specs=(anywhere, anywhere, vmem, vmem),
        scratch_shapes=[
            tall, tall, pltpu.VMEM((3, planes, nx, ny), f32), tall,
            pltpu.VMEM((planes, nx, ny), f32), pltpu.VMEM((2, nx, ny), f32),
            pltpu.VMEM((2, 4, halves, height, ny), f32), faces, faces, faces, faces,
            pltpu.VMEM((peers, 8, 128), f32), pltpu.VMEM((gz_n, 8, 128), f32),
            dma((3,)), dma((2, 4, halves)), dma((2, 4, halves)), dma((2, halves)), dma((2, halves)),
            dma((gx_n, gy_n)), dma((peers,)), dma((2, halves, gy_n)), dma((peers // 2, 2)),
            dma((peers,)), dma((peers,)), dma((gz_n,)), dma((gz_n,)),
        ],
        compiler_params=pltpu.CompilerParams(
            collective_id=0, has_side_effects=True, vmem_limit_bytes=12 * (energy.size + flow.size)
        ),
    )(energy, flow)
    count = planes * peers
    return tuple(pl.pallas_call(
        functools.partial(finish_kernel, planes),
        out_shape=(
            jax.ShapeDtypeStruct((count, height, width), f32),
            jax.ShapeDtypeStruct((count,), f32),
            jax.ShapeDtypeStruct((count,), f32),
        ),
        in_specs=[vmem] * 4,
        out_specs=(pl.BlockSpec(memory_space=pltpu.HBM), vmem, vmem),
        scratch_shapes=[pltpu.VMEM((peers // 2, planes, height, width), f32), dma((peers // 2, 2))],
        compiler_params=pltpu.CompilerParams(vmem_limit_bytes=12 * (energy.size + flow.size)),
    )(base, corr, means, running))


def per_device(energy, flow):
    gx_n, gy_n, gz_n = (lax.axis_size(a) for a in ("gx", "gy", "gz"))
    planes, nx, ny = energy.shape
    if planes > 1 and gx_n % 2 == 0 and gz_n > 1:
        return by_parity(energy, flow)
    peers = gx_n * gy_n
    parts = (1 if planes > 2 else 0) + (2 if planes > 1 else 1)
    dma = pltpu.SemaphoreType.DMA
    f32 = jnp.float32
    anywhere = pl.BlockSpec(memory_space=pl.ANY)
    vmem = pl.BlockSpec(memory_space=pltpu.VMEM)
    tall = pltpu.VMEM((planes + 2, nx + 2 * PAD, ny), f32)
    energy_next, means, running = pl.pallas_call(
        functools.partial(kernel, (gx_n, gy_n, gz_n, planes, nx, ny)),
        out_shape=(
            jax.ShapeDtypeStruct((planes * peers, nx // gx_n, ny // gy_n), f32),
            jax.ShapeDtypeStruct((8, 128), f32),
            jax.ShapeDtypeStruct((8, 128), f32),
        ),
        in_specs=[anywhere, anywhere],
        out_specs=(anywhere, vmem, vmem),
        scratch_shapes=[
            tall, tall, pltpu.VMEM((3, planes, nx, ny), f32), tall,
            pltpu.VMEM((planes, nx, ny), f32),
            pltpu.VMEM((peers, 8, 128), f32), pltpu.VMEM((gz_n, 8, 128), f32),
            dma((3,)), dma((gy_n, 4)), dma((gy_n, 4)), dma((gy_n, 2)), dma((gy_n, 2)),
            dma((peers, parts)), dma((peers, parts)), dma((parts,)),
            dma((peers,)), dma((peers,)), dma((gz_n,)), dma((gz_n,)),
        ],
        compiler_params=pltpu.CompilerParams(collective_id=0, has_side_effects=True),
    )(energy, flow)
    count = planes * peers
    return energy_next, means[0, :count], running[0, :count]


def solution(mesh):
    placed = (P(("gz", "gy", "gx"), None, None), P(None, ("gz", "gy", "gx"), None, None))
    return jax.shard_map(
        per_device,
        mesh=mesh,
        in_specs=placed,
        out_specs=(P("gz", "gx", "gy"), P("gz"), P("gz")),
        check_vma=False,
    )
```

profile of v0, /device:TPU:0, one launch (start us, length us, event | category | flops | bytes accessed | tf_op | source)
XLA Modules:
  0.0 54.0 jit_solution(15671510501751161951)
XLA Ops:
  0.6 51.8 %shard_map.49 = (f32[32,64,128]{2,1,0:T(8,128)S(1)}, f32[4,2,64,128]{3,2,1,0:T(8,128)S(1)}, f32[8,128]{1,0:T(8,128)S(1)}, f32[8,128]{1,0:T(8,128)S(1)}) custom-call(f32[4,256,256]{2,1,0:T(8,128)} %e_hbm.1, f32[4,4,256,256]{3,2,1,0:T(8,128)} %f_hbm.1), custom_call_target="tpu_custom_call" | custom-call | tf_op jit(solution)/shard_map/pallas_call | solution.py:668
  52.4 1.6 %shard_map.50 = (f32[32,64,128]{2,1,0:T(8,128)}, f32[32]{0:T(128)}, f32[32]{0:T(128)}) custom-call(f32[32,64,128]{2,1,0:T(8,128)S(1)} %get-tuple-element.7.base_ref, f32[4,2,64,128]{3,2,1,0:T(8,128)S(1)} %get-tuple-element.8.corr_ref, f32[8,128]{1,0:T(8,128)S(1)} %get-tuple-element.9.mean_in, f32[8,128]{1,0:T(8,128)S(1)} %get-tuple-element.10.run_in), custom_call_target="tpu_custom_call" | custom-call | tf_op jit(solution)/shard_map/pallas_call | solution.py:692
where the time goes:
time: 54.1 us; the launch traced here: 54 us
  Pallas kernels  53.3 us (99%)
  between operations  0.64 us (1%)
    pallas_call x1, Pallas kernels, by_parity(): pl.pallas_call(functools.partial(split_kernel, (gx_n, gy_n, gz_n, planes,...  51.8 us
    pallas_call x1, Pallas kernels, by_parity(): pl.pallas_call(functools.partial(finish_kernel, planes), out_shape=(jax.S...  1.55 us

commit v1 on v0

--- a/solution.py
+++ b/solution.py
@@ -303,14 +303,15 @@
             copy.wait_send()
 
 
-def split_kernel(
+def face_kernel(
     sizes, e_hbm, f_hbm, out, corr, mean_ref, run_ref,
     e_v, k_v, u_v, h_v, n_v, g_v, rx_v, d_v, c_v, near_v, far_v, group_v, block_v,
-    load_sem, s1, r1, s2, r2, s3, r3, sc, rc, s4, r4, s5, r5,
+    load_sem, s1, r1, s2, r2, s3, r3, sc, rc, s4, r4, s5, r5, higher, lower_sem,
 ):
     gx_n, gy_n, gz_n, planes, nx, ny = sizes
     height, width = nx // gx_n, ny // gy_n
     halves = gx_n // 2
+    deep = planes // 2
     gx, gy, gz = lax.axis_index("gx"), lax.axis_index("gy"), lax.axis_index("gz")
     peers = gx_n * gy_n
     count = peers * planes
@@ -318,9 +319,7 @@
     slab = gz * peers + place
     parity = lax.rem(gx, 2)
     total = peers * gz_n
-    above_slab, below_slab = lax.rem(slab + 1, total), lax.rem(slab + total - 1, total)
     last = planes - 1
-    own_plane = (0, last)
 
     def device(number):
         return {
@@ -329,34 +328,57 @@
             "gz": lax.div(number, peers),
         }
 
-    neighbour = (device(below_slab), device(above_slab))
-
     def peer(step):
         return device(gz * peers + lax.rem(place + step, peers))
 
     def layer(step):
         return {"gx": gx, "gy": gy, "gz": lax.rem(gz + step, gz_n)}
 
-    loads = [
-        pltpu.make_async_copy(e_hbm, e_v.at[:, pl.ds(PAD, nx)], load_sem.at[0]),
-        pltpu.make_async_copy(f_hbm.at[3], k_v.at[:, pl.ds(PAD, nx)], load_sem.at[1]),
-        pltpu.make_async_copy(f_hbm.at[pl.ds(0, 3)], u_v, load_sem.at[2]),
+    side = (1 - parity, parity)
+    sign = tuple((1 - 2 * s).astype(jnp.float32) for s in side)
+    far_slab = tuple(lax.rem(slab + total + 2 * s - 1, total) for s in side)
+    neighbour = tuple(device(s) for s in far_slab)
+    group = tuple(s * deep for s in side)
+
+    def plane(w, t):
+        return t + side[w] * (last - 2 * t)
+
+    half_row = lax.div(gx, 2)
+
+    def turn(first, i):
+        return lax.rem(first + 1 + i, halves)
+
+    theirs = [2 * turn(half_row, i) + 1 - parity for i in range(halves)]
+    mine = [
+        [2 * turn(lax.div(lax.rem(far_slab[w], gx_n), 2), i) + parity for i in range(halves)] for w in (0, 1)
     ]
-    for load in loads:
-        load.start()
+
+    loads = []
+    for w in (0, 1):
+        some = pl.ds(group[w], deep)
+        loads.append([
+            pltpu.make_async_copy(e_hbm.at[some], e_v.at[some, pl.ds(PAD, nx)], load_sem.at[w, 0]),
+            pltpu.make_async_copy(f_hbm.at[3, some], k_v.at[some, pl.ds(PAD, nx)], load_sem.at[w, 1]),
+            pltpu.make_async_copy(f_hbm.at[pl.ds(0, 3), some], u_v.at[:, some], load_sem.at[w, 2]),
+        ])
 
     barrier = pltpu.get_barrier_semaphore()
-    greet = list(neighbour) + [peer(i) for i in range(1, peers)] + [layer(i) for i in range(1, gz_n)]
-    greet.append(device(lax.rem(gz + gz_n - 1, gz_n) * peers + peers - 1))
-    greet.append(device(lax.rem(gz + 1, gz_n) * peers))
-    for target in greet:
-        pl.semaphore_signal(barrier, inc=1, device_id=target, device_id_type=MESH)
+    for i in range(1, peers):
+        pl.semaphore_signal(barrier, inc=1, device_id=peer(i), device_id_type=MESH)
+    for i in range(1, gz_n):
+
+        @pl.when(gz + i < gz_n)
+        def _():
+            pl.semaphore_signal(barrier, inc=1, device_id=layer(i), device_id_type=MESH)
+
+    for w in (0, 1):
+        for load in loads[w]:
+            load.start()
     edge = jnp.zeros((planes, PAD, ny), jnp.float32)
     for ref in (e_v, k_v, h_v):
         ref[:, 0:PAD, :] = edge
         ref[:, PAD + nx : PAD + nx + PAD, :] = edge
-    outermost = (place == 0).astype(jnp.int32) + (place == peers - 1).astype(jnp.int32)
-    pl.semaphore_wait(barrier, len(greet) - 2 + outermost * peers)
+    pl.semaphore_wait(barrier, peers - 1 + gz)
 
     def lanes(c):
         return pl.ds(c * width, width)
@@ -370,29 +392,31 @@
     def row(block, extra=0):
         return pl.multiple_of(block * height + extra, 8)
 
-    mine = [2 * j + parity for j in range(halves)]
-    theirs = [2 * j + 1 - parity for j in range(halves)]
-
     first = {}
 
-    def start_first(j, fields):
-        for f in (1, 0):
-            p, rows = own_plane[f], pl.ds(row(theirs[j]), height)
-            inner = pl.ds(row(theirs[j], PAD), height)
-            sources = (e_hbm.at[p, rows], f_hbm.at[3, p, rows], g_v.at[f, rows], h_v.at[p, inner])
-            for i in fields:
-                copy = send(sources[i], rx_v.at[1 - f, i, j], s1.at[f, i, j], r1.at[1 - f, i, j], neighbour[f])
-                copy.start()
-                first[f, i, j] = copy
-
-    start_first(0, (0, 1))
-    for load in loads:
-        load.wait()
+    def start_first(w, i, fields):
+        p, rows = plane(w, 0), pl.ds(row(theirs[i]), height)
+        inner = pl.ds(row(theirs[i], PAD), height)
+        sources = (e_hbm.at[p, rows], f_hbm.at[3, p, rows], g_v.at[w, rows], h_v.at[p, inner])
+        for field in fields:
+            copy = send(
+                sources[field], rx_v.at[w, field, i], s1.at[w, field, i], r1.at[w, field, i], neighbour[w]
+            )
+            copy.start()
+            first[w, field, i] = copy
+
+    for i in range(halves):
+        start_first(0, i, (0, 1))
+    for i in range(1, gz_n):
+
+        @pl.when(gz - i >= 0)
+        def _():
+            pl.semaphore_signal(higher, inc=1, device_id=layer(gz_n - i), device_id_type=MESH)
 
     lane = lax.broadcasted_iota(jnp.int32, (ROWS, ny), 1)
     tiles = height // ROWS
 
-    def local(src, p, start):
+    def inplane(src, p, start):
         here = pl.ds(start, ROWS)
         inner = pl.ds(pl.multiple_of(start + PAD, 8), ROWS)
         tall = pl.ds(start, ROWS + 2 * PAD)
@@ -404,12 +428,20 @@
         k_next, k_prev = sideways(k, lane)
         speed = u_v[2, p, here, :]
         value = value + above(k, k_next, speed, e, e_next) + below(k, k_prev, speed, e, e_prev)
-        speed = u_v[0, p, here, :]
-        if p < last:
-            value = value + above(k, k_v[p + 1, inner, :], speed, e, src[p + 1, inner, :])
-        if p > 0:
-            value = value + below(k, k_v[p - 1, inner, :], speed, e, src[p - 1, inner, :])
-        return here, inner, value, 0.5 * k, speed
+        return here, inner, value, e, k, u_v[0, p, here, :]
+
+    def at_face(src, w, start):
+        p, q = plane(w, 0), plane(w, 1)
+        here, inner, value, e, k, speed = inplane(src, p, start)
+        speed = sign[w] * speed
+        value = value + below(k, k_v[q, inner, :], -speed, e, src[q, inner, :])
+        return here, inner, value, k, speed
+
+    def inside(src, p, start):
+        here, inner, value, e, k, speed = inplane(src, p, start)
+        value = value + above(k, k_v[p + 1, inner, :], speed, e, src[p + 1, inner, :])
+        value = value + below(k, k_v[p - 1, inner, :], speed, e, src[p - 1, inner, :])
+        return here, inner, value
 
     def folded(value):
         part = value[0:8]
@@ -417,105 +449,77 @@
             part = part + value[i : i + 8]
         return part
 
-    def first_step(block, which):
+    def first_face(w, block):
         @pl.loop(0, tiles)
         def _(t):
             start = pl.multiple_of(block * height + t * ROWS, 8)
-            for p in which:
-                here, inner, value, half, speed = local(e_v, p, start)
-                h_v[p, inner, :] = value
-                if p == 0:
-                    g_v[0, here, :] = half + jnp.maximum(speed, 0.0)
-                if p == last:
-                    g_v[1, here, :] = half - jnp.minimum(speed, 0.0)
-
-    for j in range(halves):
-        if j > 0:
-            start_first(j, (0, 1))
-        first_step(theirs[j], own_plane)
-        start_first(j, (2, 3))
-    for j in range(halves):
-        first_step(mine[j], own_plane)
-    inside = tuple(range(1, last))
-    if inside:
-        for block in range(gx_n):
-            first_step(block, inside)
-
-    second, fixes = [], []
-    side_slab = (below_slab, above_slab)
+            here, inner, value, k, speed = at_face(e_v, w, start)
+            h_v[plane(w, 0), inner, :] = value
+            g_v[w, here, :] = 0.5 * k + jnp.maximum(speed, 0.0)
+
+    def first_faces(w):
+        for load in loads[w]:
+            load.wait()
+        for i in range(halves):
+            first_face(w, theirs[i])
+            start_first(w, i, (2, 3))
+
+    first_faces(0)
+
+    @pl.when(gz < gz_n - 1)
+    def _():
+        pl.semaphore_wait(higher, gz_n - 1 - gz)
+
+    for i in range(1, gz_n):
+
+        @pl.when(gz + i < gz_n)
+        def _():
+            pl.semaphore_signal(lower_sem, inc=1, device_id=layer(i), device_id_type=MESH)
+
+    @pl.when(gz > 0)
+    def _():
+        pl.semaphore_wait(lower_sem, gz)
+
+    for i in range(halves):
+        start_first(1, i, (0, 1))
+    first_faces(1)
+    for w in (0, 1):
+        for i in range(halves):
+            first_face(w, mine[w][i])
+    for p in range(1, last):
+
+        @pl.loop(0, nx // ROWS)
+        def _(t, p=p):
+            here, inner, value = inside(e_v, p, pl.multiple_of(t * ROWS, 8))
+            h_v[p, inner, :] = value
+
     zero = jnp.zeros((8, ny), jnp.float32)
-    spill = (zero, zero)
-    sums = [zero] * planes
-
-    def second_step(block, j, own, p, low, high):
-        def body(t, carry):
-            start = pl.multiple_of(block * height + t * ROWS, 8)
-            at = pl.ds(pl.multiple_of(t * ROWS, 8), ROWS)
-            here, inner, value, half, speed = local(h_v, p, start)
-            for f in (0, 1):
-                if own and p == own_plane[f]:
-                    value = value + near_v[f, j, at, :]
-            n_v[p, here, :] = value
+    spill = [zero, zero]
+    sums = [[zero] * deep for _ in (0, 1)]
+    second = []
+
+    def second_step(w, t, block, i, low, high):
+        def body(r, carry):
+            start = pl.multiple_of(block * height + r * ROWS, 8)
+            if t == 0:
+                here, inner, value, k, speed = at_face(h_v, w, start)
+                if i is not None:
+                    value = value + near_v[w, i, pl.ds(pl.multiple_of(r * ROWS, 8), ROWS), :]
+            else:
+                here, inner, value = inside(h_v, plane(w, t), start)
+            n_v[plane(w, t), here, :] = value
             return carry + folded(value)
 
-        sums[p] = lax.fori_loop(low, high, body, sums[p])
-
-    def ahead(j):
-        for p in range(planes):
-            inside = 0 < p < last
-            second_step(mine[j], j, 1, p, 0 if inside else 1, tiles if inside else tiles - 1)
-
-    def behind(j):
-        for p in own_plane:
+        sums[w][t] = lax.fori_loop(low, high, body, sums[w][t])
+
+    def ahead(w, i):
+        for t in range(deep):
+            second_step(w, t, mine[w][i], i, 0 if t else 1, tiles if t else tiles - 1)
+
+    def behind(w):
+        for i in range(halves):
             for t in sorted({0, tiles - 1}):
-                second_step(mine[j], j, 1, p, t, t + 1)
-
-    for j in range(halves):
-        for f in (0, 1):
-            for i in range(4):
-                send(rx_v.at[f, i, j], rx_v.at[f, i, j], s1.at[f, i, j], r1.at[f, i, j], neighbour[f]).wait_recv()
-
-        def body(t, carry, j=j):
-            sums = []
-            at = pl.ds(pl.multiple_of(t * ROWS, 8), ROWS)
-            start = pl.multiple_of(mine[j] * height + t * ROWS, 8)
-            here, inner = pl.ds(start, ROWS), pl.ds(pl.multiple_of(start + PAD, 8), ROWS)
-            for f in (0, 1):
-                p = own_plane[f]
-                to_near = g_v[f, here, :] + 0.5 * rx_v[f, 1, j, at, :]
-                to_far = rx_v[f, 2, j, at, :] + 0.5 * k_v[p, inner, :]
-                step = rx_v[f, 0, j, at, :] - e_v[p, inner, :]
-                push = to_far * step
-                d_v[f, j, at, :] = -push
-                here_half = h_v[p, inner, :] + to_near * step
-                far_half = rx_v[f, 3, j, at, :] - push
-                h_v[p, inner, :] = here_half
-                step = far_half - here_half
-                near_v[f, j, at, :] = to_near * step
-                fix = -(to_far * step)
-                far_v[f, j, at, :] = fix
-                sums.append(carry[f] + folded(fix))
-            return tuple(sums)
-
-        spill = lax.fori_loop(0, tiles, body, spill)
-        for f in (1, 0):
-            copy = send(d_v.at[f, j], c_v.at[1 - f, j], s2.at[f, j], r2.at[1 - f, j], neighbour[f])
-            copy.start()
-            second.append(copy)
-        if j < halves - 1:
-            ahead(j)
-
-    def fix_copies(act):
-        for j in range(halves):
-            for f in (0, 1):
-                far_place, far_block = lax.rem(side_slab[f], peers), lax.div(side_slab[f], peers)
-                slot = lax.div(far_place, 2)
-                for c in range(gy_n):
-                    at_home = (mine[j] == gx) & (gy == c) & (far_block == gz)
-                    act(
-                        at_home, far_v.at[f, j, :, lanes(c)], corr.at[slot, 1 - f], sc.at[f, j, c],
-                        rc.at[slot, 1 - f], {"gx": mine[j], "gy": jnp.int32(c), "gz": far_block},
-                    )
+                second_step(w, 0, mine[w][i], i, t, t + 1)
 
     def begin(at_home, src, dst, send_sem, recv_sem, target):
         @pl.when(at_home)
@@ -531,53 +535,112 @@
         def _():
             send(src, dst, send_sem, recv_sem, target).wait_send()
 
-    fix_copies(begin)
-    ahead(halves - 1)
-
-    def hand_out(block, j, own, act):
+    def fix_copies(w, i, act):
+        far_place, far_block = lax.rem(far_slab[w], peers), lax.div(far_slab[w], peers)
+        slot = lax.div(far_place, 2)
+        block = mine[w][i]
+        for c in range(gy_n):
+            at_home = (block == gx) & (gy == c) & (far_block == gz)
+            act(
+                at_home, far_v.at[w, i, :, lanes(c)], corr.at[slot, 1 - side[w]], sc.at[w, i, c],
+                rc.at[slot, 1 - side[w]], {"gx": block, "gy": jnp.int32(c), "gz": far_block},
+            )
+
+    def hand_out(w, block, index, act):
         for c in range(gy_n):
             at_home = (block == gx) & (gy == c)
             act(
-                at_home, n_v.at[:, pl.ds(row(block), height), lanes(c)], out.at[pl.ds(place * planes, planes)],
-                s3.at[2 * j + own, c], r3.at[place], {"gx": block, "gy": jnp.int32(c), "gz": gz},
+                at_home, n_v.at[pl.ds(group[w], deep), pl.ds(row(block), height), lanes(c)],
+                out.at[pl.ds(place * planes + group[w], deep)],
+                s3.at[w, index, c], r3.at[place], {"gx": block, "gy": jnp.int32(c), "gz": gz},
             )
 
-    for j in range(halves):
-        for f in (0, 1):
-            first[f, 3, j].wait_send()
-            send(d_v.at[f, j], c_v.at[f, j], s2.at[f, j], r2.at[f, j], neighbour[f]).wait_recv()
+    def meet(w, i):
+        for field in range(4):
+            send(
+                rx_v.at[w, field, i], rx_v.at[w, field, i], s1.at[w, field, i], r1.at[w, field, i], neighbour[w]
+            ).wait_recv()
+        p = plane(w, 0)
+
+        def body(t, carry):
+            at = pl.ds(pl.multiple_of(t * ROWS, 8), ROWS)
+            start = pl.multiple_of(mine[w][i] * height + t * ROWS, 8)
+            here, inner = pl.ds(start, ROWS), pl.ds(pl.multiple_of(start + PAD, 8), ROWS)
+            to_near = g_v[w, here, :] + 0.5 * rx_v[w, 1, i, at, :]
+            to_far = rx_v[w, 2, i, at, :] + 0.5 * k_v[p, inner, :]
+            step = rx_v[w, 0, i, at, :] - e_v[p, inner, :]
+            push = to_far * step
+            d_v[w, i, at, :] = -push
+            here_half = h_v[p, inner, :] + to_near * step
+            far_half = rx_v[w, 3, i, at, :] - push
+            h_v[p, inner, :] = here_half
+            step = far_half - here_half
+            near_v[w, i, at, :] = to_near * step
+            fix = -(to_far * step)
+            far_v[w, i, at, :] = fix
+            return carry + folded(fix)
+
+        spill[w] = lax.fori_loop(0, tiles, body, spill[w])
+        copy = send(d_v.at[w, i], c_v.at[w, i], s2.at[w, i], r2.at[w, i], neighbour[w])
+        copy.start()
+        second.append(copy)
+        fix_copies(w, i, begin)
+
+    def give(w, i):
+        first[w, 3, i].wait_send()
+        send(d_v.at[w, i], c_v.at[w, i], s2.at[w, i], r2.at[w, i], neighbour[w]).wait_recv()
+        p = plane(w, 0)
 
         @pl.loop(0, tiles)
-        def _(t, j=j):
+        def _(t):
             at = pl.ds(pl.multiple_of(t * ROWS, 8), ROWS)
-            inner = pl.ds(pl.multiple_of(theirs[j] * height + t * ROWS + PAD, 8), ROWS)
-            for f in (0, 1):
-                h_v[own_plane[f], inner, :] = h_v[own_plane[f], inner, :] + c_v[f, j, at, :]
-
-        for p in range(planes):
-            second_step(theirs[j], j, 0, p, 0, tiles)
-        if j < halves - 1:
-            hand_out(theirs[j], j, 0, begin)
-    for j in range(halves):
-        behind(j)
+            inner = pl.ds(pl.multiple_of(theirs[i] * height + t * ROWS + PAD, 8), ROWS)
+            h_v[p, inner, :] = h_v[p, inner, :] + c_v[w, i, at, :]
+
+        for t in range(deep):
+            second_step(w, t, theirs[i], None, 0, tiles)
+
+    def hand_theirs(w, i, act):
+        hand_out(w, theirs[i], i, act)
+
+    def hand_mine(w, act):
+        for i in range(halves):
+            hand_out(w, mine[w][i], halves + i, act)
+
+    for i in range(halves):
+        meet(0, i)
+        ahead(0, i)
+    for i in range(halves):
+        meet(1, i)
+        if i < halves - 1:
+            ahead(1, i)
+    for i in range(halves):
+        give(0, i)
+        hand_theirs(0, i, begin)
+    behind(0)
+    hand_mine(0, begin)
+    ahead(1, halves - 1)
+    for i in range(halves):
+        give(1, i)
+    behind(1)
 
     spot = lax.broadcasted_iota(jnp.int32, (8, 128), 1)
     scale = 1.0 / (nx * ny)
     part = jnp.zeros((8, 128), jnp.float32)
     base = place * planes
-    amounts = [jnp.sum(spill[0], keepdims=True)] + [jnp.sum(s, keepdims=True) for s in sums]
-    amounts.append(jnp.sum(spill[1], keepdims=True))
-    for i, amount in enumerate(amounts):
-        part = jnp.where(spot == base + i, amount * scale, part)
+    for w in (0, 1):
+        part = jnp.where(spot == base + side[w] * (planes + 1), jnp.sum(spill[w], keepdims=True) * scale, part)
+        for t in range(deep):
+            part = jnp.where(spot == base + 1 + plane(w, t), jnp.sum(sums[w][t], keepdims=True) * scale, part)
     group_v[0] = part
     share = []
     for i in range(1, peers):
         copy = send(group_v.at[0], group_v.at[i], s4.at[i], r4.at[i], peer(i))
         copy.start()
         share.append(copy)
-    hand_out(theirs[-1], halves - 1, 0, begin)
-    for j in range(halves):
-        hand_out(mine[j], j, 1, begin)
+    for i in range(halves):
+        hand_theirs(1, i, begin)
+    hand_mine(1, begin)
     for copy in share:
         copy.wait_recv()
     for i in range(1, peers):
@@ -616,14 +679,15 @@
 
     for s in range(peers):
         dst = out.at[pl.ds(s * planes, planes)]
-        send(dst, dst, s3.at[0, 0], r3.at[s], neighbour[0]).wait_recv()
+        send(dst, dst, s3.at[0, 0, 0], r3.at[s], neighbour[0]).wait_recv()
     for slot in range(peers // 2):
         for f in (0, 1):
             send(corr.at[slot, f], corr.at[slot, f], sc.at[0, 0, 0], rc.at[slot, f], neighbour[0]).wait_recv()
-    for j in range(halves):
-        hand_out(theirs[j], j, 0, finish)
-        hand_out(mine[j], j, 1, finish)
-    fix_copies(finish)
+    for w in (0, 1):
+        for i in range(halves):
+            hand_theirs(w, i, finish)
+            fix_copies(w, i, finish)
+        hand_mine(w, finish)
     for key, copy in first.items():
         if key[1] != 3:
             copy.wait_send()
@@ -666,7 +730,7 @@
     faces = pltpu.VMEM((2, halves, height, ny), f32)
     energy, flow = (pltpu.with_memory_space_constraint(x, pltpu.HBM) for x in (energy, flow))
     base, corr, means, running = pl.pallas_call(
-        functools.partial(split_kernel, (gx_n, gy_n, gz_n, planes, nx, ny)),
+        functools.partial(face_kernel, (gx_n, gy_n, gz_n, planes, nx, ny)),
         out_shape=(
             jax.ShapeDtypeStruct((planes * peers, height, width), f32),
             jax.ShapeDtypeStruct((peers // 2, 2, height, width), f32),
@@ -680,9 +744,10 @@
             pltpu.VMEM((planes, nx, ny), f32), pltpu.VMEM((2, nx, ny), f32),
             pltpu.VMEM((2, 4, halves, height, ny), f32), faces, faces, faces, faces,
             pltpu.VMEM((peers, 8, 128), f32), pltpu.VMEM((gz_n, 8, 128), f32),
-            dma((3,)), dma((2, 4, halves)), dma((2, 4, halves)), dma((2, halves)), dma((2, halves)),
-            dma((gx_n, gy_n)), dma((peers,)), dma((2, halves, gy_n)), dma((peers // 2, 2)),
+            dma((2, 3)), dma((2, 4, halves)), dma((2, 4, halves)), dma((2, halves)), dma((2, halves)),
+            dma((2, gx_n, gy_n)), dma((peers,)), dma((2, halves, gy_n)), dma((peers // 2, 2)),
             dma((peers,)), dma((peers,)), dma((gz_n,)), dma((gz_n,)),
+            pltpu.SemaphoreType.REGULAR, pltpu.SemaphoreType.REGULAR,
         ],
         compiler_params=pltpu.CompilerParams(
             collective_id=0, has_side_effects=True, vmem_limit_bytes=12 * (energy.size + flow.size)
@@ -706,7 +771,7 @@
 def per_device(energy, flow):
     gx_n, gy_n, gz_n = (lax.axis_size(a) for a in ("gx", "gy", "gz"))
     planes, nx, ny = energy.shape
-    if planes > 1 and gx_n % 2 == 0 and gz_n > 1:
+    if planes > 3 and planes % 2 == 0 and gx_n % 2 == 0 and gz_n > 1:
         return by_parity(energy, flow)
     peers = gx_n * gy_n
     parts = (1 if planes > 2 else 0) + (2 if planes > 1 else 1)

time: 54.1 us -> 52.5 us (0.970)
  Pallas kernels: 53.3 us -> 51.7 us
    pallas_call x1, Pallas kernels: 51.8 us -> 50.1 us  [by_parity(): pl.pallas_call(functools.partial(face_kernel, (gx_n, gy_n, gz_n, planes,...]
where the time goes in v1:
time: 52.5 us; the launch traced here: 52.3 us
  Pallas kernels  51.7 us (98%)
  between operations  0.64 us (1%)
    pallas_call x1, Pallas kernels, by_parity(): pl.pallas_call(functools.partial(face_kernel, (gx_n, gy_n, gz_n, planes,...  50.1 us
    pallas_call x1, Pallas kernels, by_parity(): pl.pallas_call(functools.partial(finish_kernel, planes), out_shape=(jax.S...  1.55 us

profile of v1, /device:TPU:0, one launch (start us, length us, event | category | flops | bytes accessed | tf_op | source)
XLA Modules:
  0.0 52.3 jit_solution(2863708003916487724)
XLA Ops:
  0.6 50.1 %shard_map.49 = (f32[32,64,128]{2,1,0:T(8,128)S(1)}, f32[4,2,64,128]{3,2,1,0:T(8,128)S(1)}, f32[8,128]{1,0:T(8,128)S(1)}, f32[8,128]{1,0:T(8,128)S(1)}) custom-call(f32[4,256,256]{2,1,0:T(8,128)} %e_hbm.1, f32[4,4,256,256]{3,2,1,0:T(8,128)} %f_hbm.1), custom_call_target="tpu_custom_call" | custom-call | tf_op jit(solution)/shard_map/pallas_call | solution.py:732
  50.8 1.6 %shard_map.50 = (f32[32,64,128]{2,1,0:T(8,128)}, f32[32]{0:T(128)}, f32[32]{0:T(128)}) custom-call(f32[32,64,128]{2,1,0:T(8,128)S(1)} %get-tuple-element.7.base_ref, f32[4,2,64,128]{3,2,1,0:T(8,128)S(1)} %get-tuple-element.8.corr_ref, f32[8,128]{1,0:T(8,128)S(1)} %get-tuple-element.9.mean_in, f32[8,128]{1,0:T(8,128)S(1)} %get-tuple-element.10.run_in), custom_call_target="tpu_custom_call" | custom-call | tf_op jit(solution)/shard_map/pallas_call | solution.py:757

commit v2 on v1

--- a/solution.py
+++ b/solution.py
@@ -304,9 +304,9 @@
 
 
 def face_kernel(
-    sizes, e_hbm, f_hbm, out, corr, mean_ref, run_ref,
-    e_v, k_v, u_v, h_v, n_v, g_v, rx_v, d_v, c_v, near_v, far_v, group_v, block_v,
-    load_sem, s1, r1, s2, r2, s3, r3, sc, rc, s4, r4, s5, r5, higher, lower_sem,
+    sizes, e_hbm, f_hbm, out, mean_ref, run_ref,
+    x_v, h_v, n_v, g_v, rx_v, d_v, c_v, near_v, far_v, corr, spill_v, fixed_v, group_v, block_v,
+    load_sem, s1, r1, s2, r2, s3, r3, s4, r4, s5, r5, s6, r6, s7, r7, known, higher, lower,
 ):
     gx_n, gy_n, gz_n, planes, nx, ny = sizes
     height, width = nx // gx_n, ny // gy_n
@@ -340,6 +340,9 @@
     neighbour = tuple(device(s) for s in far_slab)
     group = tuple(s * deep for s in side)
 
+    crossing = lax.div(far_slab[1], peers) != gz
+    e_v, k_v = x_v.at[0], x_v.at[1]
+
     def plane(w, t):
         return t + side[w] * (last - 2 * t)
 
@@ -357,14 +360,17 @@
     for w in (0, 1):
         some = pl.ds(group[w], deep)
         loads.append([
-            pltpu.make_async_copy(e_hbm.at[some], e_v.at[some, pl.ds(PAD, nx)], load_sem.at[w, 0]),
-            pltpu.make_async_copy(f_hbm.at[3, some], k_v.at[some, pl.ds(PAD, nx)], load_sem.at[w, 1]),
-            pltpu.make_async_copy(f_hbm.at[pl.ds(0, 3), some], u_v.at[:, some], load_sem.at[w, 2]),
+            pltpu.make_async_copy(e_hbm.at[some], x_v.at[0, some, pl.ds(PAD, nx)], load_sem.at[w]),
+            pltpu.make_async_copy(f_hbm.at[3, some], x_v.at[1, some, pl.ds(PAD, nx)], load_sem.at[w]),
+            pltpu.make_async_copy(f_hbm.at[pl.ds(0, 3), some], x_v.at[pl.ds(2, 3), some, pl.ds(PAD, nx)], load_sem.at[w]),
         ])
 
     barrier = pltpu.get_barrier_semaphore()
-    for i in range(1, peers):
-        pl.semaphore_signal(barrier, inc=1, device_id=peer(i), device_id_type=MESH)
+    near = [{"gx": gx + 1 - 2 * parity, "gy": gy, "gz": gz}]
+    near += [{"gx": lax.rem(gx + 2 * i, gx_n), "gy": gy, "gz": gz} for i in range(1, halves)]
+    near += [{"gx": gx, "gy": lax.rem(gy + i, gy_n), "gz": gz} for i in range(1, gy_n)]
+    for target in near:
+        pl.semaphore_signal(barrier, inc=1, device_id=target, device_id_type=MESH)
     for i in range(1, gz_n):
 
         @pl.when(gz + i < gz_n)
@@ -375,10 +381,15 @@
         for load in loads[w]:
             load.start()
     edge = jnp.zeros((planes, PAD, ny), jnp.float32)
-    for ref in (e_v, k_v, h_v):
+    for ref in (x_v.at[0], x_v.at[1], h_v):
         ref[:, 0:PAD, :] = edge
         ref[:, PAD + nx : PAD + nx + PAD, :] = edge
-    pl.semaphore_wait(barrier, peers - 1 + gz)
+    block_v[...] = jnp.zeros(block_v.shape, jnp.float32)
+
+    def entry_barrier():
+        pl.semaphore_wait(barrier, len(near) + gz)
+
+    entry_barrier()
 
     def lanes(c):
         return pl.ds(c * width, width)
@@ -392,26 +403,17 @@
     def row(block, extra=0):
         return pl.multiple_of(block * height + extra, 8)
 
-    first = {}
-
     def start_first(w, i, fields):
         p, rows = plane(w, 0), pl.ds(row(theirs[i]), height)
         inner = pl.ds(row(theirs[i], PAD), height)
         sources = (e_hbm.at[p, rows], f_hbm.at[3, p, rows], g_v.at[w, rows], h_v.at[p, inner])
         for field in fields:
-            copy = send(
-                sources[field], rx_v.at[w, field, i], s1.at[w, field, i], r1.at[w, field, i], neighbour[w]
-            )
-            copy.start()
-            first[w, field, i] = copy
+            send(sources[field], rx_v.at[w, i, field], s1.at[w], r1.at[w, i], neighbour[w]).start()
 
     for i in range(halves):
         start_first(0, i, (0, 1))
-    for i in range(1, gz_n):
-
-        @pl.when(gz - i >= 0)
-        def _():
-            pl.semaphore_signal(higher, inc=1, device_id=layer(gz_n - i), device_id_type=MESH)
+    for target in near:
+        pl.semaphore_signal(known.at[0], inc=1, device_id=target, device_id_type=MESH)
 
     lane = lax.broadcasted_iota(jnp.int32, (ROWS, ny), 1)
     tiles = height // ROWS
@@ -422,13 +424,13 @@
         tall = pl.ds(start, ROWS + 2 * PAD)
         e, e_next, e_prev = shifted(src[p, tall, :], ROWS)
         k, k_next, k_prev = shifted(k_v[p, tall, :], ROWS)
-        speed = u_v[1, p, here, :]
+        speed = x_v[3, p, inner, :]
         value = e + above(k, k_next, speed, e, e_next) + below(k, k_prev, speed, e, e_prev)
         e_next, e_prev = sideways(e, lane)
         k_next, k_prev = sideways(k, lane)
-        speed = u_v[2, p, here, :]
+        speed = x_v[4, p, inner, :]
         value = value + above(k, k_next, speed, e, e_next) + below(k, k_prev, speed, e, e_prev)
-        return here, inner, value, e, k, u_v[0, p, here, :]
+        return here, inner, value, e, k, x_v[2, p, inner, :]
 
     def at_face(src, w, start):
         p, q = plane(w, 0), plane(w, 1)
@@ -457,46 +459,68 @@
             h_v[plane(w, 0), inner, :] = value
             g_v[w, here, :] = 0.5 * k + jnp.maximum(speed, 0.0)
 
-    def first_faces(w):
-        for load in loads[w]:
-            load.wait()
-        for i in range(halves):
-            first_face(w, theirs[i])
-            start_first(w, i, (2, 3))
-
-    first_faces(0)
-
-    @pl.when(gz < gz_n - 1)
+    def hear_higher():
+        @pl.when(gz < gz_n - 1)
+        def _():
+            pl.semaphore_wait(higher, gz_n - 1 - gz)
+
+        for i in range(1, gz_n):
+
+            @pl.when(gz + i < gz_n)
+            def _():
+                pl.semaphore_signal(lower, inc=1, device_id=layer(i), device_id_type=MESH)
+
+    def hear_lower():
+        @pl.when(gz > 0)
+        def _():
+            pl.semaphore_wait(lower, gz)
+
+    def land(w):
+        some = x_v.at[:, pl.ds(group[w], deep), pl.ds(PAD, nx)]
+        pltpu.make_async_copy(some, some, load_sem.at[w]).wait()
+
+    land(0)
+    first_face(0, theirs[0])
+    start_first(0, 0, (2, 3))
+    pl.semaphore_wait(known.at[0], len(near))
+    for target in near:
+        pl.semaphore_signal(known.at[1], inc=1, device_id=target, device_id_type=MESH)
+    for i in range(1, halves):
+        first_face(0, theirs[i])
+        start_first(0, i, (2, 3))
+    land(1)
+    first_face(1, theirs[0])
+    pl.semaphore_wait(known.at[1], len(near))
+    for i in range(1, gz_n):
+
+        @pl.when(gz - i >= 0)
+        def _():
+            pl.semaphore_signal(higher, inc=1, device_id=layer(gz_n - i), device_id_type=MESH)
+
+
+    @pl.when(jnp.logical_not(crossing))
     def _():
-        pl.semaphore_wait(higher, gz_n - 1 - gz)
-
-    for i in range(1, gz_n):
-
-        @pl.when(gz + i < gz_n)
-        def _():
-            pl.semaphore_signal(lower_sem, inc=1, device_id=layer(i), device_id_type=MESH)
-
-    @pl.when(gz > 0)
-    def _():
-        pl.semaphore_wait(lower_sem, gz)
-
-    for i in range(halves):
-        start_first(1, i, (0, 1))
-    first_faces(1)
+        start_first(1, 0, (0, 1, 2, 3))
+
+    for i in range(1, halves):
+        first_face(1, theirs[i])
     for w in (0, 1):
         for i in range(halves):
             first_face(w, mine[w][i])
-    for p in range(1, last):
-
-        @pl.loop(0, nx // ROWS)
-        def _(t, p=p):
-            here, inner, value = inside(e_v, p, pl.multiple_of(t * ROWS, 8))
-            h_v[p, inner, :] = value
+    def inner_planes():
+        for p in range(1, last):
+
+            @pl.loop(0, nx // ROWS)
+            def _(t, p=p):
+                here, inner, value = inside(e_v, p, pl.multiple_of(t * ROWS, 8))
+                h_v[p, inner, :] = value
+
+    inner_planes()
+    hear_higher()
 
     zero = jnp.zeros((8, ny), jnp.float32)
     spill = [zero, zero]
     sums = [[zero] * deep for _ in (0, 1)]
-    second = []
 
     def second_step(w, t, block, i, low, high):
         def body(r, carry):
@@ -530,49 +554,34 @@
         def _():
             send(src, dst, send_sem, recv_sem, target).start()
 
-    def finish(at_home, src, dst, send_sem, recv_sem, target):
-        @pl.when(jnp.logical_not(at_home))
-        def _():
-            send(src, dst, send_sem, recv_sem, target).wait_send()
-
-    def fix_copies(w, i, act):
+    def fix_copies(w, i):
         far_place, far_block = lax.rem(far_slab[w], peers), lax.div(far_slab[w], peers)
         slot = lax.div(far_place, 2)
         block = mine[w][i]
         for c in range(gy_n):
             at_home = (block == gx) & (gy == c) & (far_block == gz)
-            act(
-                at_home, far_v.at[w, i, :, lanes(c)], corr.at[slot, 1 - side[w]], sc.at[w, i, c],
-                rc.at[slot, 1 - side[w]], {"gx": block, "gy": jnp.int32(c), "gz": far_block},
+            begin(
+                at_home, far_v.at[w, i, :, lanes(c)], corr.at[slot, 1 - side[w]], s4, r4,
+                {"gx": block, "gy": jnp.int32(c), "gz": far_block},
             )
 
-    def hand_out(w, block, index, act):
-        for c in range(gy_n):
-            at_home = (block == gx) & (gy == c)
-            act(
-                at_home, n_v.at[pl.ds(group[w], deep), pl.ds(row(block), height), lanes(c)],
-                out.at[pl.ds(place * planes + group[w], deep)],
-                s3.at[w, index, c], r3.at[place], {"gx": block, "gy": jnp.int32(c), "gz": gz},
-            )
-
-    def meet(w, i):
-        for field in range(4):
-            send(
-                rx_v.at[w, field, i], rx_v.at[w, field, i], s1.at[w, field, i], r1.at[w, field, i], neighbour[w]
-            ).wait_recv()
+    def meet_wait(w, i):
+        send(rx_v.at[w, i], rx_v.at[w, i], s1.at[w], r1.at[w, i], neighbour[w]).wait_recv()
+
+    def meet_calc(w, i):
         p = plane(w, 0)
 
         def body(t, carry):
             at = pl.ds(pl.multiple_of(t * ROWS, 8), ROWS)
             start = pl.multiple_of(mine[w][i] * height + t * ROWS, 8)
             here, inner = pl.ds(start, ROWS), pl.ds(pl.multiple_of(start + PAD, 8), ROWS)
-            to_near = g_v[w, here, :] + 0.5 * rx_v[w, 1, i, at, :]
-            to_far = rx_v[w, 2, i, at, :] + 0.5 * k_v[p, inner, :]
-            step = rx_v[w, 0, i, at, :] - e_v[p, inner, :]
+            to_near = g_v[w, here, :] + 0.5 * rx_v[w, i, 1, at, :]
+            to_far = rx_v[w, i, 2, at, :] + 0.5 * k_v[p, inner, :]
+            step = rx_v[w, i, 0, at, :] - e_v[p, inner, :]
             push = to_far * step
             d_v[w, i, at, :] = -push
             here_half = h_v[p, inner, :] + to_near * step
-            far_half = rx_v[w, 3, i, at, :] - push
+            far_half = rx_v[w, i, 3, at, :] - push
             h_v[p, inner, :] = here_half
             step = far_half - here_half
             near_v[w, i, at, :] = to_near * step
@@ -581,14 +590,24 @@
             return carry + folded(fix)
 
         spill[w] = lax.fori_loop(0, tiles, body, spill[w])
-        copy = send(d_v.at[w, i], c_v.at[w, i], s2.at[w, i], r2.at[w, i], neighbour[w])
-        copy.start()
-        second.append(copy)
-        fix_copies(w, i, begin)
-
-    def give(w, i):
-        first[w, 3, i].wait_send()
-        send(d_v.at[w, i], c_v.at[w, i], s2.at[w, i], r2.at[w, i], neighbour[w]).wait_recv()
+
+    def meet_send(w, i):
+        send(d_v.at[w, i], c_v.at[w, i], s2, r2.at[w, i], neighbour[w]).start()
+        fix_copies(w, i)
+
+    def spill_copy(w):
+        return send(spill_v.at[w], fixed_v.at[w], s5, r5, neighbour[w])
+
+    def spill_out(w):
+        spill_v[w] = jnp.broadcast_to(jnp.sum(spill[w], keepdims=True), (8, 128))
+        spill_copy(w).start()
+
+    def give_wait(w, i):
+        if i == 0:
+            send(rx_v.at[w], rx_v.at[w], s1.at[w], r1.at[w, 0], neighbour[w]).wait_send()
+        send(d_v.at[w, i], c_v.at[w, i], s2, r2.at[w, i], neighbour[w]).wait_recv()
+
+    def give_calc(w, i):
         p = plane(w, 0)
 
         @pl.loop(0, tiles)
@@ -600,114 +619,174 @@
         for t in range(deep):
             second_step(w, t, theirs[i], None, 0, tiles)
 
-    def hand_theirs(w, i, act):
-        hand_out(w, theirs[i], i, act)
-
-    def hand_mine(w, act):
+    def hand_theirs(w, i):
+        for c in range(gy_n):
+            send(
+                n_v.at[pl.ds(group[w], deep), pl.ds(row(theirs[i]), height), lanes(c)],
+                out.at[pl.ds(place * planes + group[w], deep)], s3, r3,
+                {"gx": theirs[i], "gy": jnp.int32(c), "gz": gz},
+            ).start()
+
+    def mine_piece(w, i, p, some, start, rows):
+        for c in range(gy_n):
+            at_home = (mine[w][i] == gx) & (gy == c)
+            begin(
+                at_home,
+                n_v.at[pl.ds(p, some), pl.ds(row(mine[w][i], start), rows), lanes(c)],
+                out.at[pl.ds(place * planes + p, some), pl.ds(start, rows)],
+                s3, r3, {"gx": mine[w][i], "gy": jnp.int32(c), "gz": gz},
+            )
+
+    def mine_early(w, i):
+        mine_piece(w, i, group[w] + 1 - side[w], deep - 1, 0, height)
+        mine_piece(w, i, plane(w, 0), 1, ROWS, height - 2 * ROWS)
+
+    def mine_late(w):
         for i in range(halves):
-            hand_out(w, mine[w][i], halves + i, act)
+            mine_piece(w, i, plane(w, 0), 1, 0, ROWS)
+            mine_piece(w, i, plane(w, 0), 1, height - ROWS, ROWS)
 
     for i in range(halves):
-        meet(0, i)
+        meet_wait(0, i)
+        meet_calc(0, i)
+        meet_send(0, i)
+    hear_lower()
+
+    @pl.when(crossing)
+    def _():
+        start_first(1, 0, (0, 1, 2, 3))
+
+    for i in range(1, halves):
+        start_first(1, i, (0, 1, 2, 3))
+    spill_out(0)
+    for i in range(halves):
         ahead(0, i)
+        mine_early(0, i)
     for i in range(halves):
-        meet(1, i)
+        meet_wait(1, i)
+        meet_calc(1, i)
+        meet_send(1, i)
         if i < halves - 1:
             ahead(1, i)
+            mine_early(1, i)
+    spill_out(1)
     for i in range(halves):
-        give(0, i)
-        hand_theirs(0, i, begin)
+        give_wait(0, i)
+        give_calc(0, i)
+        hand_theirs(0, i)
     behind(0)
-    hand_mine(0, begin)
+    mine_late(0)
     ahead(1, halves - 1)
+    mine_early(1, halves - 1)
     for i in range(halves):
-        give(1, i)
+        give_wait(1, i)
+        give_calc(1, i)
     behind(1)
 
     spot = lax.broadcasted_iota(jnp.int32, (8, 128), 1)
     scale = 1.0 / (nx * ny)
     part = jnp.zeros((8, 128), jnp.float32)
-    base = place * planes
+    send(spill_v, fixed_v, s5, r5, neighbour[0]).wait_recv()
     for w in (0, 1):
-        part = jnp.where(spot == base + side[w] * (planes + 1), jnp.sum(spill[w], keepdims=True) * scale, part)
         for t in range(deep):
-            part = jnp.where(spot == base + 1 + plane(w, t), jnp.sum(sums[w][t], keepdims=True) * scale, part)
+            amount = jnp.sum(sums[w][t], keepdims=True)
+            if t == 0:
+                amount = amount + fixed_v[w]
+            part = jnp.where(spot == place * planes + plane(w, t), amount * scale, part)
     group_v[0] = part
-    share = []
     for i in range(1, peers):
-        copy = send(group_v.at[0], group_v.at[i], s4.at[i], r4.at[i], peer(i))
-        copy.start()
-        share.append(copy)
+        send(group_v.at[0], group_v.at[i], s6, r6, peer(i)).start()
     for i in range(halves):
-        hand_theirs(1, i, begin)
-    hand_mine(1, begin)
-    for copy in share:
-        copy.wait_recv()
+        hand_theirs(1, i)
+    mine_late(1)
+
+    others = group_v.at[pl.ds(1, peers - 1)]
+
+    def early_sends():
+        send(d_v, c_v, s2, r2.at[0, 0], neighbour[0]).wait_send()
+        send(spill_v, fixed_v, s5, r5, neighbour[0]).wait_send()
+
+    def share_wait():
+        send(others, others, s6, r6, neighbour[0]).wait_recv()
+
+    early_sends()
+    share_wait()
     for i in range(1, peers):
         part = part + group_v[i]
     block_v[0] = part
-    climb = []
+
+    def climb_copy(i):
+        return send(block_v.at[0], block_v.at[i], s7, r7, layer(i))
+
     for i in range(1, gz_n):
-        copy = send(block_v.at[0], block_v.at[i], s5.at[i], r5.at[i], layer(i))
-        copy.start()
-        climb.append(copy)
-    for copy in climb:
-        copy.wait_recv()
-    lower = jnp.zeros((8, 128), jnp.float32)
-    own_lane = (spot >= 1) & (spot <= count)
-    means = jnp.where(own_lane, part, 0.0)
-    for i in range(gz_n):
-        vector = block_v[i]
-        block = lax.rem(gz + gz_n - i, gz_n)
-        owner = jnp.where(own_lane, block, jnp.where(
-            spot == 0, lax.rem(block + gz_n - 1, gz_n), lax.rem(block + 1, gz_n)))
-        vector = jnp.where(spot <= count + 1, vector, 0.0)
-        lower = lower + jnp.where(owner < gz, vector, 0.0)
-        low = jnp.sum(jnp.where((spot == 0) & (owner == gz), vector, 0.0)[0:1], axis=1, keepdims=True)
-        high = jnp.sum(jnp.where((spot == count + 1) & (owner == gz), vector, 0.0)[0:1], axis=1, keepdims=True)
-        means = means + jnp.where(spot == count, low, 0.0) + jnp.where(spot == 1, high, 0.0)
-    means = pltpu.roll(means, 127, 1)
-    running = means
+
+        @pl.when(gz + i < gz_n)
+        def _():
+            climb_copy(i).start()
+
+    running = part
     step = 1
     while step < count:
         running = running + jnp.where(spot >= step, pltpu.roll(running, step, 1), 0.0)
         step *= 2
-    mean_ref[...] = means
-    offset = jnp.sum(lower[0:1], axis=1, keepdims=True)
+    mean_ref[...] = part
+
+    def climb_all():
+        for i in range(1, gz_n):
+
+            @pl.when(gz == i)
+            def _():
+                some = block_v.at[pl.ds(1, i)]
+                send(some, some, s7, r7, layer(1)).wait_recv()
+
+    climb_all()
+    under = block_v[1]
+    for i in range(2, gz_n):
+        under = under + block_v[i]
+    offset = jnp.sum(jnp.where(spot < count, under, 0.0)[0:1], axis=1, keepdims=True)
     rank = (gz * count + spot + 1).astype(jnp.float32)
     run_ref[...] = (running + offset) / rank
 
-    for s in range(peers):
-        dst = out.at[pl.ds(s * planes, planes)]
-        send(dst, dst, s3.at[0, 0, 0], r3.at[s], neighbour[0]).wait_recv()
+    def final_out():
+        send(out, out, s3, r3, neighbour[0]).wait_recv()
+
+    def final_corr():
+        send(corr, corr, s4, r4, neighbour[0]).wait_recv()
+
+    final_corr()
+    final_out()
     for slot in range(peers // 2):
-        for f in (0, 1):
-            send(corr.at[slot, f], corr.at[slot, f], sc.at[0, 0, 0], rc.at[slot, f], neighbour[0]).wait_recv()
-    for w in (0, 1):
-        for i in range(halves):
-            hand_theirs(w, i, finish)
-            fix_copies(w, i, finish)
-        hand_mine(w, finish)
-    for key, copy in first.items():
-        if key[1] != 3:
-            copy.wait_send()
-    for copy in second + share + climb:
-        copy.wait_send()
-
-
-def finish_kernel(planes, base_ref, corr_ref, mean_in, run_in, out_ref, mean_ref, run_ref, fix_v, done):
-    other = 1 - lax.rem(lax.axis_index("gx"), 2)
+        start = (2 * slot + 1 - parity) * planes
+        for f, p in ((0, 0), (1, last)):
+            out[start + p] = out[start + p] + corr[slot, f]
+
+    def final_sends():
+        some = out.at[pl.ds(0, (peers - 1) * planes)]
+        send(some, some, s3, r3, neighbour[0]).wait_send()
+        send(others, others, s6, r6, neighbour[0]).wait_send()
+        for n in (0, 1):
+
+            @pl.when(crossing == bool(n))
+            def _():
+                some = out.at[pl.ds(0, 2 * (halves * gy_n - 1) + n)]
+                send(some, some, s4, r4, neighbour[0]).wait_send()
+
+        for i in range(1, gz_n):
+
+            @pl.when(gz == gz_n - 1 - i)
+            def _():
+                some = block_v.at[pl.ds(0, i)]
+                send(some, some, s7, r7, layer(1)).wait_send()
+
+    final_sends()
+
+
+def finish_kernel(base_ref, mean_in, run_in, out_ref, mean_ref, run_ref, done):
+    rows = base_ref.shape[0] // 4
     copies = []
-    for slot in range(corr_ref.shape[0]):
-        whole = pl.ds((2 * slot + 1 - other) * planes, planes)
-        copies.append(pltpu.make_async_copy(base_ref.at[whole], out_ref.at[whole], done.at[slot, 0]))
-        copies[-1].start()
-    for slot in range(corr_ref.shape[0]):
-        start = (2 * slot + other) * planes
-        fix_v[slot] = base_ref[pl.ds(start, planes)]
-        for f, p in ((0, 0), (1, planes - 1)):
-            fix_v[slot, p] = fix_v[slot, p] + corr_ref[slot, f]
-        copies.append(pltpu.make_async_copy(fix_v.at[slot], out_ref.at[pl.ds(start, planes)], done.at[slot, 1]))
+    for i in range(4):
+        some = pl.ds(i * rows, rows)
+        copies.append(pltpu.make_async_copy(base_ref.at[some], out_ref.at[some], done.at[i]))
         copies[-1].start()
     count = mean_ref.shape[0]
     mean_ref[...] = mean_in[0, 0:count]
@@ -716,38 +795,36 @@
         copy.wait()
 
 
-def by_parity(energy, flow):
+def by_faces(energy, flow):
     gx_n, gy_n, gz_n = (lax.axis_size(a) for a in ("gx", "gy", "gz"))
     planes, nx, ny = energy.shape
     peers, halves = gx_n * gy_n, gx_n // 2
     height, width = nx // gx_n, ny // gy_n
-    dma = pltpu.SemaphoreType.DMA
+    dma, regular = pltpu.SemaphoreType.DMA, pltpu.SemaphoreType.REGULAR
     f32 = jnp.float32
-    anywhere = pl.BlockSpec(memory_space=pl.ANY)
     vmem = pl.BlockSpec(memory_space=pltpu.VMEM)
-    tall = pltpu.VMEM((planes, nx + 2 * PAD, ny), f32)
     hbm = pl.BlockSpec(memory_space=pltpu.HBM)
     faces = pltpu.VMEM((2, halves, height, ny), f32)
     energy, flow = (pltpu.with_memory_space_constraint(x, pltpu.HBM) for x in (energy, flow))
-    base, corr, means, running = pl.pallas_call(
+    base, means, running = pl.pallas_call(
         functools.partial(face_kernel, (gx_n, gy_n, gz_n, planes, nx, ny)),
         out_shape=(
             jax.ShapeDtypeStruct((planes * peers, height, width), f32),
-            jax.ShapeDtypeStruct((peers // 2, 2, height, width), f32),
             jax.ShapeDtypeStruct((8, 128), f32),
             jax.ShapeDtypeStruct((8, 128), f32),
         ),
         in_specs=[hbm, hbm],
-        out_specs=(anywhere, anywhere, vmem, vmem),
+        out_specs=(vmem, vmem, vmem),
         scratch_shapes=[
-            tall, tall, pltpu.VMEM((3, planes, nx, ny), f32), tall,
+            pltpu.VMEM((5, planes, nx + 2 * PAD, ny), f32), pltpu.VMEM((planes, nx + 2 * PAD, ny), f32),
             pltpu.VMEM((planes, nx, ny), f32), pltpu.VMEM((2, nx, ny), f32),
-            pltpu.VMEM((2, 4, halves, height, ny), f32), faces, faces, faces, faces,
+            pltpu.VMEM((2, halves, 4, height, ny), f32), faces, faces, faces, faces,
+            pltpu.VMEM((peers // 2, 2, height, width), f32),
+            pltpu.VMEM((2, 8, 128), f32), pltpu.VMEM((2, 8, 128), f32),
             pltpu.VMEM((peers, 8, 128), f32), pltpu.VMEM((gz_n, 8, 128), f32),
-            dma((2, 3)), dma((2, 4, halves)), dma((2, 4, halves)), dma((2, halves)), dma((2, halves)),
-            dma((2, gx_n, gy_n)), dma((peers,)), dma((2, halves, gy_n)), dma((peers // 2, 2)),
-            dma((peers,)), dma((peers,)), dma((gz_n,)), dma((gz_n,)),
-            pltpu.SemaphoreType.REGULAR, pltpu.SemaphoreType.REGULAR,
+            dma((2,)), dma((2,)), dma((2, halves)), dma, dma((2, halves)),
+            dma, dma, dma, dma, dma, dma, dma, dma, dma, dma,
+            regular((2,)), regular, regular,
         ],
         compiler_params=pltpu.CompilerParams(
             collective_id=0, has_side_effects=True, vmem_limit_bytes=12 * (energy.size + flow.size)
@@ -755,24 +832,24 @@
     )(energy, flow)
     count = planes * peers
     return tuple(pl.pallas_call(
-        functools.partial(finish_kernel, planes),
+        finish_kernel,
         out_shape=(
             jax.ShapeDtypeStruct((count, height, width), f32),
             jax.ShapeDtypeStruct((count,), f32),
             jax.ShapeDtypeStruct((count,), f32),
         ),
-        in_specs=[vmem] * 4,
+        in_specs=[vmem] * 3,
         out_specs=(pl.BlockSpec(memory_space=pltpu.HBM), vmem, vmem),
-        scratch_shapes=[pltpu.VMEM((peers // 2, planes, height, width), f32), dma((peers // 2, 2))],
+        scratch_shapes=[dma((4,))],
         compiler_params=pltpu.CompilerParams(vmem_limit_bytes=12 * (energy.size + flow.size)),
-    )(base, corr, means, running))
+    )(base, means, running))
 
 
 def per_device(energy, flow):
     gx_n, gy_n, gz_n = (lax.axis_size(a) for a in ("gx", "gy", "gz"))
     planes, nx, ny = energy.shape
     if planes > 3 and planes % 2 == 0 and gx_n % 2 == 0 and gz_n > 1:
-        return by_parity(energy, flow)
+        return by_faces(energy, flow)
     peers = gx_n * gy_n
     parts = (1 if planes > 2 else 0) + (2 if planes > 1 else 1)
     dma = pltpu.SemaphoreType.DMA

time: 52.5 us -> 48.8 us (0.930)
  Pallas kernels: 51.7 us -> 48 us
    pallas_call x2, Pallas kernels: 51.7 us -> 48 us  [the longest x1 46.5 us: by_faces(): pl.pallas_call(functools.partial(face_kernel, (gx_n, gy_n, gz_n, planes,...]
where the time goes in v2:
time: 48.8 us; the launch traced here: 48.6 us
  Pallas kernels  48 us (98%)
  between operations  0.64 us (1%)
    pallas_call x1, Pallas kernels, by_faces(): pl.pallas_call(functools.partial(face_kernel, (gx_n, gy_n, gz_n, planes,...  46.5 us
    pallas_call x1, Pallas kernels, by_faces(): pl.pallas_call(finish_kernel, out_shape=(jax.ShapeDtypeStruct((count, hei...  1.51 us

profile of v2, /device:TPU:0, one launch (start us, length us, event | category | flops | bytes accessed | tf_op | source)
XLA Modules:
  0.0 48.6 jit_solution(8945821587694661319)
XLA Ops:
  0.6 46.5 %shard_map.49 = (f32[32,64,128]{2,1,0:T(8,128)S(1)}, f32[8,128]{1,0:T(8,128)S(1)}, f32[8,128]{1,0:T(8,128)S(1)}) custom-call(f32[4,256,256]{2,1,0:T(8,128)} %e_hbm.1, f32[4,4,256,256]{3,2,1,0:T(8,128)} %f_hbm.1), custom_call_target="tpu_custom_call" | custom-call | tf_op jit(solution)/shard_map/pallas_call | solution.py:809
  47.1 1.5 %shard_map.50 = (f32[32,64,128]{2,1,0:T(8,128)}, f32[32]{0:T(128)}, f32[32]{0:T(128)}) custom-call(f32[32,64,128]{2,1,0:T(8,128)S(1)} %get-tuple-element.6.base_ref, f32[8,128]{1,0:T(8,128)S(1)} %get-tuple-element.7.mean_in, f32[8,128]{1,0:T(8,128)S(1)} %get-tuple-element.8.run_in), custom_call_target="tpu_custom_call" | custom-call | tf_op jit(solution)/shard_map/pallas_call | solution.py:834

commit v3 on v2

--- a/solution.py
+++ b/solution.py
@@ -596,7 +596,7 @@
         fix_copies(w, i)
 
     def spill_copy(w):
-        return send(spill_v.at[w], fixed_v.at[w], s5, r5, neighbour[w])
+        return send(spill_v.at[w, pl.ds(0, 1)], fixed_v.at[w, pl.ds(0, 1)], s5, r5, neighbour[w])
 
     def spill_out(w):
         spill_v[w] = jnp.broadcast_to(jnp.sum(spill[w], keepdims=True), (8, 128))
@@ -646,36 +646,51 @@
             mine_piece(w, i, plane(w, 0), 1, 0, ROWS)
             mine_piece(w, i, plane(w, 0), 1, height - ROWS, ROWS)
 
+    def when(condition, act):
+        @pl.when(condition)
+        def _():
+            act()
+
+    inland = jnp.logical_not(crossing)
+
+    def second_faces():
+        for i in range(1, halves):
+            start_first(1, i, (0, 1, 2, 3))
+
+    def hand_first():
+        for i in range(halves - 1):
+            hand_theirs(0, i)
+
     for i in range(halves):
         meet_wait(0, i)
         meet_calc(0, i)
         meet_send(0, i)
     hear_lower()
-
-    @pl.when(crossing)
-    def _():
-        start_first(1, 0, (0, 1, 2, 3))
-
-    for i in range(1, halves):
-        start_first(1, i, (0, 1, 2, 3))
+    when(inland, second_faces)
+    when(crossing, lambda: start_first(1, 0, (0, 1, 2, 3)))
     spill_out(0)
     for i in range(halves):
         ahead(0, i)
         mine_early(0, i)
     for i in range(halves):
+        if i == halves - 1:
+            for j in range(halves):
+                give_wait(0, j)
+                give_calc(0, j)
+            when(inland, hand_first)
+            behind(0)
+            mine_late(0)
         meet_wait(1, i)
         meet_calc(1, i)
         meet_send(1, i)
+        if i == 0:
+            when(crossing, second_faces)
         if i < halves - 1:
             ahead(1, i)
             mine_early(1, i)
     spill_out(1)
-    for i in range(halves):
-        give_wait(0, i)
-        give_calc(0, i)
-        hand_theirs(0, i)
-    behind(0)
-    mine_late(0)
+    when(crossing, hand_first)
+    hand_theirs(0, halves - 1)
     ahead(1, halves - 1)
     mine_early(1, halves - 1)
     for i in range(halves):
@@ -683,28 +698,29 @@
         give_calc(1, i)
     behind(1)
 
-    spot = lax.broadcasted_iota(jnp.int32, (8, 128), 1)
+    spot = lax.broadcasted_iota(jnp.int32, (1, 128), 1)
     scale = 1.0 / (nx * ny)
-    part = jnp.zeros((8, 128), jnp.float32)
-    send(spill_v, fixed_v, s5, r5, neighbour[0]).wait_recv()
+    part = jnp.zeros((1, 128), jnp.float32)
+    spilled = spill_v.at[:, pl.ds(0, 1)]
+    send(spilled, spilled, s5, r5, neighbour[0]).wait_recv()
     for w in (0, 1):
         for t in range(deep):
             amount = jnp.sum(sums[w][t], keepdims=True)
             if t == 0:
-                amount = amount + fixed_v[w]
+                amount = amount + fixed_v[w, 0:1, 0:1]
             part = jnp.where(spot == place * planes + plane(w, t), amount * scale, part)
-    group_v[0] = part
+    group_v[0, 0:1] = part
     for i in range(1, peers):
-        send(group_v.at[0], group_v.at[i], s6, r6, peer(i)).start()
-    for i in range(halves):
+        send(group_v.at[0, pl.ds(0, 1)], group_v.at[i, pl.ds(0, 1)], s6, r6, peer(i)).start()
+    for i in reversed(range(halves)):
         hand_theirs(1, i)
     mine_late(1)
 
-    others = group_v.at[pl.ds(1, peers - 1)]
+    others = group_v.at[pl.ds(1, peers - 1), pl.ds(0, 1)]
 
     def early_sends():
         send(d_v, c_v, s2, r2.at[0, 0], neighbour[0]).wait_send()
-        send(spill_v, fixed_v, s5, r5, neighbour[0]).wait_send()
+        send(spilled, spilled, s5, r5, neighbour[0]).wait_send()
 
     def share_wait():
         send(others, others, s6, r6, neighbour[0]).wait_recv()
@@ -712,11 +728,11 @@
     early_sends()
     share_wait()
     for i in range(1, peers):
-        part = part + group_v[i]
-    block_v[0] = part
+        part = part + group_v[i, 0:1]
+    block_v[0, 0:1] = part
 
     def climb_copy(i):
-        return send(block_v.at[0], block_v.at[i], s7, r7, layer(i))
+        return send(block_v.at[0, pl.ds(0, 1)], block_v.at[i, pl.ds(0, 1)], s7, r7, layer(i))
 
     for i in range(1, gz_n):
 
@@ -729,23 +745,23 @@
     while step < count:
         running = running + jnp.where(spot >= step, pltpu.roll(running, step, 1), 0.0)
         step *= 2
-    mean_ref[...] = part
+    mean_ref[0:1] = part
 
     def climb_all():
         for i in range(1, gz_n):
 
             @pl.when(gz == i)
             def _():
-                some = block_v.at[pl.ds(1, i)]
+                some = block_v.at[pl.ds(1, i), pl.ds(0, 1)]
                 send(some, some, s7, r7, layer(1)).wait_recv()
 
     climb_all()
-    under = block_v[1]
+    under = block_v[1, 0:1]
     for i in range(2, gz_n):
-        under = under + block_v[i]
-    offset = jnp.sum(jnp.where(spot < count, under, 0.0)[0:1], axis=1, keepdims=True)
+        under = under + block_v[i, 0:1]
+    offset = jnp.sum(jnp.where(spot < count, under, 0.0), axis=1, keepdims=True)
     rank = (gz * count + spot + 1).astype(jnp.float32)
-    run_ref[...] = (running + offset) / rank
+    run_ref[0:1] = (running + offset) / rank
 
     def final_out():
         send(out, out, s3, r3, neighbour[0]).wait_recv()
@@ -775,22 +791,20 @@
 
             @pl.when(gz == gz_n - 1 - i)
             def _():
-                some = block_v.at[pl.ds(0, i)]
+                some = block_v.at[pl.ds(0, i), pl.ds(0, 1)]
                 send(some, some, s7, r7, layer(1)).wait_send()
 
     final_sends()
 
 
-def finish_kernel(base_ref, mean_in, run_in, out_ref, mean_ref, run_ref, done):
-    rows = base_ref.shape[0] // 4
-    copies = []
-    for i in range(4):
-        some = pl.ds(i * rows, rows)
-        copies.append(pltpu.make_async_copy(base_ref.at[some], out_ref.at[some], done.at[i]))
-        copies[-1].start()
+def finish_kernel(base_ref, mean_in, run_in, out_ref, mean_ref, run_ref, mean_v, run_v, done):
+    copies = [pltpu.make_async_copy(base_ref, out_ref, done.at[0])]
+    copies[0].start()
     count = mean_ref.shape[0]
-    mean_ref[...] = mean_in[0, 0:count]
-    run_ref[...] = run_in[0, 0:count]
+    for source, staged, target, i in ((mean_in, mean_v, mean_ref, 1), (run_in, run_v, run_ref, 2)):
+        staged[...] = source[0, 0:count]
+        copies.append(pltpu.make_async_copy(staged, target, done.at[i]))
+        copies[i].start()
     for copy in copies:
         copy.wait()
 
@@ -839,8 +853,8 @@
             jax.ShapeDtypeStruct((count,), f32),
         ),
         in_specs=[vmem] * 3,
-        out_specs=(pl.BlockSpec(memory_space=pltpu.HBM), vmem, vmem),
-        scratch_shapes=[dma((4,))],
+        out_specs=(hbm, hbm, hbm),
+        scratch_shapes=[pltpu.VMEM((count,), f32), pltpu.VMEM((count,), f32), dma((3,))],
         compiler_params=pltpu.CompilerParams(vmem_limit_bytes=12 * (energy.size + flow.size)),
     )(base, means, running))
 

time: 48.8 us -> 46.7 us (0.957)
  Pallas kernels: 48 us -> 45.4 us
    pallas_call x1, Pallas kernels: 46.5 us -> 44.4 us  [by_faces(): pl.pallas_call(functools.partial(face_kernel, (gx_n, gy_n, gz_n, planes,...]
    pallas_call x1, Pallas kernels: 1.51 us -> 1 us  [by_faces(): pl.pallas_call(finish_kernel, out_shape=(jax.ShapeDtypeStruct((count, hei...]
where the time goes in v3:
time: 46.7 us; the launch traced here: 46 us
  Pallas kernels  45.4 us (97%)
  between operations  0.64 us (1%)
    pallas_call x1, Pallas kernels, by_faces(): pl.pallas_call(functools.partial(face_kernel, (gx_n, gy_n, gz_n, planes,...  44.4 us
    pallas_call x1, Pallas kernels, by_faces(): pl.pallas_call(finish_kernel, out_shape=(jax.ShapeDtypeStruct((count, hei...  1 us

profile of v3, /device:TPU:0, one launch (start us, length us, event | category | flops | bytes accessed | tf_op | source)
XLA Modules:
  0.0 46.0 jit_solution(798012191123193217)
XLA Ops:
  0.6 44.4 %shard_map.49 = (f32[32,64,128]{2,1,0:T(8,128)S(1)}, f32[8,128]{1,0:T(8,128)S(1)}, f32[8,128]{1,0:T(8,128)S(1)}) custom-call(f32[4,256,256]{2,1,0:T(8,128)} %e_hbm.1, f32[4,4,256,256]{3,2,1,0:T(8,128)} %f_hbm.1), custom_call_target="tpu_custom_call" | custom-call | tf_op jit(solution)/shard_map/pallas_call | solution.py:823
  45.0 1.0 %shard_map.50 = (f32[32,64,128]{2,1,0:T(8,128)}, f32[32]{0:T(128)}, f32[32]{0:T(128)}) custom-call(f32[32,64,128]{2,1,0:T(8,128)S(1)} %get-tuple-element.6.base_ref, f32[8,128]{1,0:T(8,128)S(1)} %get-tuple-element.7.mean_in, f32[8,128]{1,0:T(8,128)S(1)} %get-tuple-element.8.run_in), custom_call_target="tpu_custom_call" | custom-call | tf_op jit(solution)/shard_map/pallas_call | solution.py:848

commit v4 on v3

--- a/solution.py
+++ b/solution.py
@@ -356,30 +356,37 @@
         [2 * turn(lax.div(lax.rem(far_slab[w], gx_n), 2), i) + parity for i in range(halves)] for w in (0, 1)
     ]
 
-    loads = []
-    for w in (0, 1):
-        some = pl.ds(group[w], deep)
-        loads.append([
-            pltpu.make_async_copy(e_hbm.at[some], x_v.at[0, some, pl.ds(PAD, nx)], load_sem.at[w]),
-            pltpu.make_async_copy(f_hbm.at[3, some], x_v.at[1, some, pl.ds(PAD, nx)], load_sem.at[w]),
-            pltpu.make_async_copy(f_hbm.at[pl.ds(0, 3), some], x_v.at[pl.ds(2, 3), some, pl.ds(PAD, nx)], load_sem.at[w]),
-        ])
+    inner = tuple(group[w] + 1 - side[w] for w in (0, 1))
+    rows_all = pl.ds(PAD, nx)
+
+    def load_planes(fields, p, some, semaphore):
+        for field in fields:
+            source = e_hbm.at[pl.ds(p, some)] if field == 0 else f_hbm.at[(field + 2) % 4, pl.ds(p, some)]
+            pltpu.make_async_copy(source, x_v.at[field, pl.ds(p, some), rows_all], load_sem.at[semaphore]).start()
+
+    def landed(first, fields, p, some, semaphore):
+        part = x_v.at[pl.ds(first, fields), pl.ds(p, some), rows_all]
+        pltpu.make_async_copy(part, part, load_sem.at[semaphore]).wait()
 
     barrier = pltpu.get_barrier_semaphore()
-    near = [{"gx": gx + 1 - 2 * parity, "gy": gy, "gz": gz}]
-    near += [{"gx": lax.rem(gx + 2 * i, gx_n), "gy": gy, "gz": gz} for i in range(1, halves)]
-    near += [{"gx": gx, "gy": lax.rem(gy + i, gy_n), "gz": gz} for i in range(1, gy_n)]
-    for target in near:
-        pl.semaphore_signal(barrier, inc=1, device_id=target, device_id_type=MESH)
-    for i in range(1, gz_n):
-
-        @pl.when(gz + i < gz_n)
+    def signal(semaphore, target):
+        pl.semaphore_signal(semaphore, inc=1, device_id=target, device_id_type=MESH)
+
+    pair = {"gx": gx + 1 - 2 * parity, "gy": gy, "gz": gz}
+    lines = [(half_row + i < halves, {"gx": lax.rem(gx + 2 * i, gx_n), "gy": gy, "gz": gz}) for i in range(1, halves)]
+    lines += [(gy - i >= 0, {"gx": gx, "gy": lax.rem(gy + gy_n - i, gy_n), "gz": gz}) for i in range(1, gy_n)]
+    earlier = half_row + gy_n - 1 - gy
+    later = halves - 1 - half_row + gy
+    signal(barrier, pair)
+    for after, target in lines + [(gz + i < gz_n, layer(i)) for i in range(1, gz_n)]:
+
+        @pl.when(after)
         def _():
-            pl.semaphore_signal(barrier, inc=1, device_id=layer(i), device_id_type=MESH)
-
-    for w in (0, 1):
-        for load in loads[w]:
-            load.start()
+            signal(barrier, target)
+
+    load_planes((0, 1), plane(0, 0), 1, 0)
+    load_planes((0, 1), inner[0], deep - 1, 1)
+    load_planes((2, 3, 4), group[0], deep, 2)
     edge = jnp.zeros((planes, PAD, ny), jnp.float32)
     for ref in (x_v.at[0], x_v.at[1], h_v):
         ref[:, 0:PAD, :] = edge
@@ -387,7 +394,7 @@
     block_v[...] = jnp.zeros(block_v.shape, jnp.float32)
 
     def entry_barrier():
-        pl.semaphore_wait(barrier, len(near) + gz)
+        pl.semaphore_wait(barrier, 1 + earlier + gz)
 
     entry_barrier()
 
@@ -403,17 +410,43 @@
     def row(block, extra=0):
         return pl.multiple_of(block * height + extra, 8)
 
-    def start_first(w, i, fields):
+    def start_first(w, i, fields, staged=False):
         p, rows = plane(w, 0), pl.ds(row(theirs[i]), height)
         inner = pl.ds(row(theirs[i], PAD), height)
         sources = (e_hbm.at[p, rows], f_hbm.at[3, p, rows], g_v.at[w, rows], h_v.at[p, inner])
+        if staged:
+            sources = (x_v.at[0, p, inner], x_v.at[1, p, inner])
         for field in fields:
             send(sources[field], rx_v.at[w, i, field], s1.at[w], r1.at[w, i], neighbour[w]).start()
 
-    for i in range(halves):
-        start_first(0, i, (0, 1))
-    for target in near:
-        pl.semaphore_signal(known.at[0], inc=1, device_id=target, device_id_type=MESH)
+    @pl.when(parity == 0)
+    def _():
+        landed(0, 2, plane(0, 0), 1, 0)
+        for i in range(halves):
+            start_first(0, i, (0, 1), True)
+
+    @pl.when(parity > 0)
+    def _():
+        for i in range(halves):
+            start_first(0, i, (0, 1))
+        landed(0, 2, plane(0, 0), 1, 0)
+
+    for after, target in lines:
+
+        @pl.when(jnp.logical_not(after))
+        def _():
+            signal(known.at[0], target)
+
+    load_planes(range(5), group[1], deep, 3)
+
+    def hear(stage, amount):
+        @pl.when(amount > 0)
+        def _():
+            pl.semaphore_wait(known.at[stage], amount)
+
+    def pass_on(stage):
+        for target in [pair] + [target for _, target in lines]:
+            signal(known.at[stage], target)
 
     lane = lax.broadcasted_iota(jnp.int32, (ROWS, ny), 1)
     tiles = height // ROWS
@@ -476,21 +509,25 @@
             pl.semaphore_wait(lower, gz)
 
     def land(w):
-        some = x_v.at[:, pl.ds(group[w], deep), pl.ds(PAD, nx)]
-        pltpu.make_async_copy(some, some, load_sem.at[w]).wait()
+        if w == 0:
+            landed(0, 2, inner[0], deep - 1, 1)
+            landed(2, 3, group[0], deep, 2)
+        else:
+            landed(0, 5, group[1], deep, 3)
 
     land(0)
     first_face(0, theirs[0])
     start_first(0, 0, (2, 3))
-    pl.semaphore_wait(known.at[0], len(near))
-    for target in near:
-        pl.semaphore_signal(known.at[1], inc=1, device_id=target, device_id_type=MESH)
+    hear(0, later)
+    pass_on(1)
     for i in range(1, halves):
         first_face(0, theirs[i])
         start_first(0, i, (2, 3))
+    hear(1, 1 + len(lines))
+    pass_on(2)
     land(1)
     first_face(1, theirs[0])
-    pl.semaphore_wait(known.at[1], len(near))
+    hear(2, 1 + len(lines))
     for i in range(1, gz_n):
 
         @pl.when(gz - i >= 0)
@@ -836,9 +873,9 @@
             pltpu.VMEM((peers // 2, 2, height, width), f32),
             pltpu.VMEM((2, 8, 128), f32), pltpu.VMEM((2, 8, 128), f32),
             pltpu.VMEM((peers, 8, 128), f32), pltpu.VMEM((gz_n, 8, 128), f32),
-            dma((2,)), dma((2,)), dma((2, halves)), dma, dma((2, halves)),
+            dma((4,)), dma((2,)), dma((2, halves)), dma, dma((2, halves)),
             dma, dma, dma, dma, dma, dma, dma, dma, dma, dma,
-            regular((2,)), regular, regular,
+            regular((3,)), regular, regular,
         ],
         compiler_params=pltpu.CompilerParams(
             collective_id=0, has_side_effects=True, vmem_limit_bytes=12 * (energy.size + flow.size)

time: 46.7 us -> 46 us (0.985)
  no operation moved by 1% of the time
where the time goes in v4:
time: 46 us; the launch traced here: 45.6 us
  Pallas kernels  45 us (98%)
  between operations  0.64 us (1%)
    pallas_call x1, Pallas kernels, by_faces(): pl.pallas_call(functools.partial(face_kernel, (gx_n, gy_n, gz_n, planes,...  43.9 us
    pallas_call x1, Pallas kernels, by_faces(): pl.pallas_call(finish_kernel, out_shape=(jax.ShapeDtypeStruct((count, hei...  1 us

profile of v4, /device:TPU:0, one launch (start us, length us, event | category | flops | bytes accessed | tf_op | source)
XLA Modules:
  0.0 45.6 jit_solution(642543818181362353)
XLA Ops:
  0.6 43.9 %shard_map.49 = (f32[32,64,128]{2,1,0:T(8,128)S(1)}, f32[8,128]{1,0:T(8,128)S(1)}, f32[8,128]{1,0:T(8,128)S(1)}) custom-call(f32[4,256,256]{2,1,0:T(8,128)} %e_hbm.1, f32[4,4,256,256]{3,2,1,0:T(8,128)} %f_hbm.1), custom_call_target="tpu_custom_call" | custom-call | tf_op jit(solution)/shard_map/pallas_call | solution.py:860
  44.6 1.0 %shard_map.50 = (f32[32,64,128]{2,1,0:T(8,128)}, f32[32]{0:T(128)}, f32[32]{0:T(128)}) custom-call(f32[32,64,128]{2,1,0:T(8,128)S(1)} %get-tuple-element.6.base_ref, f32[8,128]{1,0:T(8,128)S(1)} %get-tuple-element.7.mean_in, f32[8,128]{1,0:T(8,128)S(1)} %get-tuple-element.8.run_in), custom_call_target="tpu_custom_call" | custom-call | tf_op jit(solution)/shard_map/pallas_call | solution.py:885

commit v5 on v4

--- a/solution.py
+++ b/solution.py
@@ -571,7 +571,7 @@
             n_v[plane(w, t), here, :] = value
             return carry + folded(value)
 
-        sums[w][t] = lax.fori_loop(low, high, body, sums[w][t])
+        sums[w][t] = lax.fori_loop(low, high, body, sums[w][t], unroll=True)
 
     def ahead(w, i):
         for t in range(deep):
@@ -695,7 +695,7 @@
             start_first(1, i, (0, 1, 2, 3))
 
     def hand_first():
-        for i in range(halves - 1):
+        for i in range(1, halves):
             hand_theirs(0, i)
 
     for i in range(halves):
@@ -727,7 +727,7 @@
             mine_early(1, i)
     spill_out(1)
     when(crossing, hand_first)
-    hand_theirs(0, halves - 1)
+    hand_theirs(0, 0)
     ahead(1, halves - 1)
     mine_early(1, halves - 1)
     for i in range(halves):
@@ -749,8 +749,13 @@
     group_v[0, 0:1] = part
     for i in range(1, peers):
         send(group_v.at[0, pl.ds(0, 1)], group_v.at[i, pl.ds(0, 1)], s6, r6, peer(i)).start()
-    for i in reversed(range(halves)):
-        hand_theirs(1, i)
+    def hand_second(order):
+        for i in order:
+            hand_theirs(1, i)
+
+    between = lax.rem(gx + half_row, 2) == 1
+    when(between, lambda: hand_second(range(halves)))
+    when(jnp.logical_not(between), lambda: hand_second(reversed(range(halves))))
     mine_late(1)
 
     others = group_v.at[pl.ds(1, peers - 1), pl.ds(0, 1)]

time: 46 us -> 46.2 us (level)
  no operation moved by 1% of the time
where the time goes in v5:
time: 46.2 us; the launch traced here: 45.9 us
  Pallas kernels  45.2 us (98%)
  between operations  0.64 us (1%)
    pallas_call x1, Pallas kernels, by_faces(): pl.pallas_call(functools.partial(face_kernel, (gx_n, gy_n, gz_n, planes,...  44.2 us
    pallas_call x1, Pallas kernels, by_faces(): pl.pallas_call(finish_kernel, out_shape=(jax.ShapeDtypeStruct((count, hei...  1 us

profile of v5, /device:TPU:0, one launch (start us, length us, event | category | flops | bytes accessed | tf_op | source)
XLA Modules:
  0.0 45.9 jit_solution(8760370375052346627)
XLA Ops:
  0.6 44.2 %shard_map.49 = (f32[32,64,128]{2,1,0:T(8,128)S(1)}, f32[8,128]{1,0:T(8,128)S(1)}, f32[8,128]{1,0:T(8,128)S(1)}) custom-call(f32[4,256,256]{2,1,0:T(8,128)} %e_hbm.1, f32[4,4,256,256]{3,2,1,0:T(8,128)} %f_hbm.1), custom_call_target="tpu_custom_call" | custom-call | tf_op jit(solution)/shard_map/pallas_call | solution.py:865
  44.9 1.0 %shard_map.50 = (f32[32,64,128]{2,1,0:T(8,128)}, f32[32]{0:T(128)}, f32[32]{0:T(128)}) custom-call(f32[32,64,128]{2,1,0:T(8,128)S(1)} %get-tuple-element.6.base_ref, f32[8,128]{1,0:T(8,128)S(1)} %get-tuple-element.7.mean_in, f32[8,128]{1,0:T(8,128)S(1)} %get-tuple-element.8.run_in), custom_call_target="tpu_custom_call" | custom-call | tf_op jit(solution)/shard_map/pallas_call | solution.py:890
